TPU v7x, 128 devices: a whole 4x4x4 slice. The times are simulated.
128 devices in a mesh: edp: 2 (over z_lo), ep: 64 (over z_hi, x, y, core).
Axes of the slice: x: 4, y: 4, z: 4 (z_hi: 2, z_lo: 2; z = z_hi * 2 + z_lo), core: 2. Of those that a mesh axis runs over, the one named last changes fastest.
Arguments:
- tokens: bfloat16 [16384, 3584], P(('edp', 'ep')), may hold values from -6 to 6
- node_ids: int32 [16384, 4], P(('edp', 'ep')), may hold values from 0 to 7, as said below
- local_ids: int32 [16384, 8], P(('edp', 'ep')), may hold values from 0 to 15, as said below
- affinity: float32 [16384, 8], P(('edp', 'ep')), may hold values from 0.2 to 1
- w_gate: bfloat16 [128, 3584, 1024], P(('edp', 'ep')), may hold values from -0.09375 to 0.09375
- w_up: bfloat16 [128, 3584, 1024], P(('edp', 'ep')), may hold values from -0.09375 to 0.09375
- w_down: bfloat16 [128, 1024, 3584], P(('edp', 'ep')), may hold values from -0.1875 to 0.1875
- grad_parts: float32 [128, 3584, 128], P(('edp', 'ep')), may hold values from -2.5 to 2.5
Outputs:
- mixed: bfloat16 [16384, 3584], P(('edp', 'ep'))
- router_grad: float32 [3584, 128], P(('edp', 'ep'))
Inputs may be any that keep to these rules, and one draw needn't show every extreme that they name: `node_ids`: A token's 4 nodes are distinct and increasing. `local_ids`: columns 2 j and 2 j + 1 name the two experts 2 m and 2 m + 1 of one pair m of node node_ids[t, j], in either order. From the 128 tokens of one device each expert receives at most 10 routes; inside a node the loads from one device differ by at most one.
All inputs are finite; a program needn't handle non-finite values.
Results may differ from a plain program's by a relative error of at most 0.0057.
Values may be sent and summed in bfloat16 or wider, within the bound.
A program may use at most 192 MiB of HBM per device.

v0:
```python
import jax
import jax.numpy as jnp
from jax import lax
from jax.sharding import PartitionSpec as P

GROUPS = 8


def from_partner(block, axis, bit):
    count = lax.axis_size(axis)
    route = []
    for low in range(count):
        high = low | 1 << bit
        if high != low and high < count:
            route += [(low, high), (high, low)]
    return lax.ppermute(block, axis, route)


def split_up(array, dim, count):
    before, after = (array.shape[:dim], array.shape[dim + 1 :])
    return jnp.moveaxis(array.reshape(*before, count, -1, *after), dim, 0)


def sent_and_summed(array, axis, dim):
    parts = split_up(array, dim, lax.axis_size(axis))
    arrived = lax.all_to_all(parts, axis, split_axis=0, concat_axis=0, tiled=True)
    return arrived.astype(jnp.float32).sum(axis=0)


def sum_at_owner(array, axis, dim):
    parts = split_up(array, dim, lax.axis_size(axis))
    arrived = lax.all_to_all(parts, axis, split_axis=0, concat_axis=0, tiled=True)
    return arrived.sum(axis=0)


def body(tokens, node_ids, local_ids, affinity, w_gate, w_up, w_down, grad_parts):
    edp_count = lax.axis_size("edp")
    ep_count = lax.axis_size("ep")
    experts = edp_count * ep_count
    tok_rows, model_width = tokens.shape
    top_routes = local_ids.shape[1]
    node_pick = node_ids.shape[1]
    capacity = 10 * tok_rows // experts
    per_node = experts // GROUPS
    expert = jnp.repeat(node_ids, top_routes // node_pick, axis=1) * per_node + local_ids
    weight = 2.5 * affinity / jnp.sum(affinity, axis=1, keepdims=True)
    pair_total = experts // 2
    half_cap = (capacity + 1) // 2
    lead_expert = expert[:, 0::2]
    flat_pair = (lead_expert // 2).reshape(-1)
    pair_hot = (flat_pair[:, None] == jnp.arange(pair_total, dtype=jnp.int32)[None, :]).astype(
        jnp.int32
    )
    pair_before = jnp.cumsum(pair_hot, axis=0) - pair_hot
    pair_rank = jnp.sum(pair_before * pair_hot, axis=1)
    dest_device = 2 * flat_pair + pair_rank % 2
    pair_target = dest_device * half_cap + pair_rank // 2
    node_rows = jnp.arange(tok_rows * node_pick, dtype=jnp.int32)
    pair_owner = jnp.zeros((experts * half_cap,), jnp.int32).at[pair_target].set(node_rows + 1)
    pair_filled = pair_owner > 0
    pair_picked = tokens[jnp.maximum(pair_owner - 1, 0) // node_pick]
    pair_send = jnp.where(pair_filled[:, None], pair_picked, jnp.zeros((), jnp.bfloat16))
    pair_send = pair_send.reshape(experts, half_cap, model_width)
    own_rows = lax.all_to_all(pair_send, ("edp", "ep"), split_axis=0, concat_axis=0, tiled=True)
    partner_rows = from_partner(own_rows, "ep", 0)
    received = jnp.concatenate([own_rows, partner_rows], axis=1)
    in_shape = received.shape
    row_block = received.reshape(-1, model_width)
    gate_act = jnp.dot(row_block, w_gate[0], preferred_element_type=jnp.float32)
    up_act = jnp.dot(row_block, w_up[0], preferred_element_type=jnp.float32)
    hidden = (jax.nn.silu(gate_act) * up_act).astype(jnp.bfloat16)
    result = jnp.dot(hidden, w_down[0], preferred_element_type=jnp.float32).astype(jnp.bfloat16)
    both_out = result.reshape(in_shape)
    own_out = both_out[:, :half_cap]
    partner_out = from_partner(both_out[:, half_cap:], "ep", 0)
    back_own, back_partner = (
        lax.all_to_all(own_out, ("edp", "ep"), split_axis=0, concat_axis=0, tiled=True),
        lax.all_to_all(partner_out, ("edp", "ep"), split_axis=0, concat_axis=0, tiled=True),
    )
    back_own = back_own.reshape(experts * half_cap, model_width)[pair_target]
    back_partner = back_partner.reshape(experts * half_cap, model_width)[pair_target]
    back_own = back_own.reshape(tok_rows, node_pick, model_width)
    back_partner = back_partner.reshape(tok_rows, node_pick, model_width)
    is_own = (lead_expert == dest_device.reshape(tok_rows, node_pick))[:, :, None]
    even_out = jnp.where(is_own, back_own, back_partner)
    odd_out = jnp.where(is_own, back_partner, back_own)
    mixed_sum = jnp.zeros((tok_rows, model_width), jnp.float32)
    for column in range(node_pick):
        mixed_sum = mixed_sum + weight[:, 2 * column : 2 * column + 1] * even_out[
            :, column, :
        ].astype(jnp.float32)
        mixed_sum = mixed_sum + weight[:, 2 * column + 1 : 2 * column + 2] * odd_out[
            :, column, :
        ].astype(jnp.float32)
    half_sum = sent_and_summed(grad_parts[0].astype(jnp.bfloat16), "edp", 0)
    router_grad = sum_at_owner(half_sum, "ep", 0)
    return (mixed_sum.astype(jnp.bfloat16), router_grad)


def solution(mesh):
    placed = (
        P(("edp", "ep"), None),
        P(("edp", "ep"), None),
        P(("edp", "ep"), None),
        P(("edp", "ep"), None),
        P(("edp", "ep"), None, None),
        P(("edp", "ep"), None, None),
        P(("edp", "ep"), None, None),
        P(("edp", "ep"), None, None),
    )
    return jax.shard_map(
        body,
        mesh=mesh,
        in_specs=placed,
        out_specs=(P(("edp", "ep"), None), P(("edp", "ep"), None)),
        check_vma=False,
    )
```

profile of v0, /device:TPU:10, one launch (start us, length us, event | category | flops | bytes accessed | tf_op | source)
XLA Modules:
  0.0 513.6 jit_solution(1876373283971529542)
XLA Ops:
  2.5 1.2 reduce-window.6
  4.4 2.4 scatter_custom_fusion
  6.9 5.2 %gather_fusion = bf16[640,3584]{1,0:T(8,128)(2,1)} fusion(bf16[128,3584]{1,0:T(8,128)(2,1)S(1)} %copy-done, s32[1024]{0:T(1024)S(1)} %pad_clamp_fusion.1), kind=kCustom, calls=%fused_computation | custom fusion | bytes 9177600 | tf_op jit(solution)/shard_map/gather | solution.py:61
  12.1 7.9 %gather.12 = bf16[128,5,3584]{2,1,0:T(8,128)(2,1)} reshape(bf16[640,3584]{1,0:T(8,128)(2,1)} %gather_fusion) | data formatting | bytes 9175040 | tf_op jit(solution)/shard_map/gather | solution.py:61
  20.1 3.8 broadcast_select_fusion
  24.0 99.0 %all_to_all.25 = bf16[128,5,3584]{2,1,0:T(8,128)(2,1)S(1)} all-to-all(bf16[128,5,3584]{2,1,0:T(8,128)(2,1)S(1)} %broadcast_select_fusion), channel_id=1, replica_groups=mesh['edp'=2,'ep'=64] {'edp','ep'}, dimensions={0} | all-to-all | bytes 9175040 | tf_op jit(solution)/shard_map/all_to_all | solution.py:64
  123.0 3.6 copy.55
  127.9 15.2 %all_to_all.26 = bf16[2,1792,128]{2,1,0:T(8,128)(2,1)S(1)} all-to-all(bf16[2,1792,128]{2,1,0:T(8,128)(2,1)S(1)} %bitcast.90), channel_id=1, replica_groups=mesh['edp'=2,'ep'=64] {'edp'}, dimensions={0} | all-to-all | bytes 1835008 | tf_op jit(solution)/shard_map/all_to_all | solution.py:26
  143.3 1.0 reshape.182
  144.3 12.8 %all-to-all-start.4 = ((f32[64,28,128]{2,1,0:T(8,128)}), f32[64,28,128]{2,1,0:T(8,128)S(1)}, u32[]{:S(2)}, u32[]{:S(2)}) async-start(f32[64,28,128]{2,1,0:T(8,128)} %reshape.182), calls=%async_computation.4 | async-start | bytes 2097152 | tf_op jit(solution)/shard_map/all_to_all | solution.py:32
  157.1 4.9 copy.56
  162.0 11.9 %pad_maximum_fusion = bf16[128,10,3584]{2,1,0:T(8,128)(2,1)} fusion(bf16[128,5,3584]{2,1,0:T(8,128)(2,1)S(1)} %copy.56, bf16[128,5,3584]{2,1,0:T(8,128)(2,1)} %copy-done.2), kind=kLoop, calls=%fused_computation.5 | loop fusion | flops 18350080 | bytes 18350080 | tf_op jit(solution)/shard_map/concatenate | solution.py:66
  173.9 14.6 %reshape.176 = bf16[1280,3584]{1,0:T(8,128)(2,1)} reshape(bf16[128,10,3584]{2,1,0:T(8,128)(2,1)} %pad_maximum_fusion) | data formatting | bytes 18350080 | tf_op jit(solution)/shard_map/reshape | solution.py:68
  188.5 13.7 %fusion.1 = f32[1280,1024]{1,0:T(8,128)S(1)} fusion(bf16[1280,3584]{1,0:T(8,128)(2,1)} %reshape.176, bf16[1,3584,1024]{2,1,0:T(8,128)(2,1)} %param.13), kind=kOutput, calls=%fused_computation.7 | convolution fusion | flops 9395240960 | bytes 21757952 | tf_op jit(solution)/shard_map/dot_general | solution.py:70
  202.2 13.6 %fusion.3 = f32[1280,1024]{1,0:T(8,128)} fusion(bf16[1280,3584]{1,0:T(8,128)(2,1)S(1)} %copy-done.3, bf16[1,3584,1024]{2,1,0:T(8,128)(2,1)} %param.12), kind=kOutput, calls=%fused_computation.9 | convolution fusion | flops 9395240960 | bytes 21757952 | tf_op jit(solution)/shard_map/dot_general | solution.py:69
  215.8 16.3 %convolution_convert_fusion = bf16[1280,3584]{1,0:T(8,128)(2,1)} fusion(bf16[1,1024,3584]{2,1,0:T(8,128)(2,1)S(1)} %bitcast.96, f32[1280,1024]{1,0:T(8,128)S(1)} %fusion.1, f32[1280,1024]{1,0:T(8,128)} %fusion.3), kind=kOutput, calls=%fused_computation.4 | convolution fusion | flops 9407692800 | bytes 27000832 | tf_op jit(solution)/shard_map/dot_general | solution.py:72
  232.2 14.2 %reshape.177 = bf16[128,10,3584]{2,1,0:T(8,128)(2,1)} reshape(bf16[1280,3584]{1,0:T(8,128)(2,1)} %convolution_convert_fusion) | data formatting | bytes 18350080 | tf_op jit(solution)/shard_map/reshape | solution.py:73
  246.4 10.5 %fusion.28 = (bf16[128,5,3584]{2,1,0:T(8,128)(2,1)}, bf16[128,5,3584]{2,1,0:T(8,128)(2,1)S(1)}) fusion(bf16[128,10,3584]{2,1,0:T(8,128)(2,1)} %reshape.177), kind=kLoop, calls=%fused_computation.94 | loop fusion | bytes 18350080 | tf_op jit(solution)/shard_map/slice | solution.py:74
  256.9 3.6 copy.57
  260.7 9.9 %all-to-all-start.1 = ((bf16[128,5,3584]{2,1,0:T(8,128)(2,1)}), bf16[128,5,3584]{2,1,0:T(8,128)(2,1)}, u32[]{:S(2)}, u32[]{:S(2)}) async-start(bf16[128,5,3584]{2,1,0:T(8,128)(2,1)} %get-tuple-element.4), calls=%async_computation.1 | async-start | bytes 14680064 | tf_op jit(solution)/shard_map/all_to_all | solution.py:77
  270.5 7.9 %copy.58 = bf16[128,5,3584]{2,1,0:T(8,128)(2,1)} copy(bf16[128,5,3584]{2,0,1:T(8,128)(2,1)} %collective-permute-done.1) | data formatting | bytes 9175040 | tf_op jit(solution)/shard_map/ppermute | solution.py:16
  278.4 92.3 %all-to-all-done.1 = bf16[128,5,3584]{2,1,0:T(8,128)(2,1)} async-done(((bf16[128,5,3584]{2,1,0:T(8,128)(2,1)}), bf16[128,5,3584]{2,1,0:T(8,128)(2,1)}, u32[]{:S(2)}, u32[]{:S(2)}) %all-to-all-start.1) | async-done | bytes 4587552 | tf_op jit(solution)/shard_map/all_to_all | solution.py:77
  370.7 5.2 %all-to-all-start.2 = ((bf16[128,5,3584]{2,1,0:T(8,128)(2,1)}), bf16[128,5,3584]{2,1,0:T(8,128)(2,1)}, u32[]{:S(2)}, u32[]{:S(2)}) async-start(bf16[128,5,3584]{2,1,0:T(8,128)(2,1)} %copy.58), calls=%async_computation.2 | async-start | bytes 14680064 | tf_op jit(solution)/shard_map/all_to_all | solution.py:78
  376.9 8.1 %reshape.178 = bf16[640,3584]{1,0:T(8,128)(2,1)} reshape(bf16[128,5,3584]{2,1,0:T(8,128)(2,1)} %all-to-all-done.1) | data formatting | bytes 9175040 | tf_op jit(solution)/shard_map/reshape | solution.py:80
  384.9 10.8 %gather_fusion.1 = bf16[512,3584]{1,0:T(8,128)(2,1)} fusion(bf16[640,3584]{1,0:T(8,128)(2,1)} %reshape.178, s32[1024]{0:T(1024)S(1)} %pad_clamp_fusion), kind=kCustom, calls=%fused_computation.1 | custom fusion | bytes 7342080 | tf_op jit(solution)/shard_map/gather | solution.py:80
  395.7 7.0 %reshape.179 = bf16[128,4,3584]{2,1,0:T(4,128)(2,1)} reshape(bf16[512,3584]{1,0:T(8,128)(2,1)} %gather_fusion.1) | data formatting | bytes 7340032 | tf_op jit(solution)/shard_map/reshape | solution.py:82
  402.8 74.3 %all-to-all-done.2 = bf16[128,5,3584]{2,1,0:T(8,128)(2,1)} async-done(((bf16[128,5,3584]{2,1,0:T(8,128)(2,1)}), bf16[128,5,3584]{2,1,0:T(8,128)(2,1)}, u32[]{:S(2)}, u32[]{:S(2)}) %all-to-all-start.2) | async-done | bytes 4587552 | tf_op jit(solution)/shard_map/all_to_all | solution.py:78
  477.1 8.1 %reshape.180 = bf16[640,3584]{1,0:T(8,128)(2,1)} reshape(bf16[128,5,3584]{2,1,0:T(8,128)(2,1)} %all-to-all-done.2) | data formatting | bytes 9175040 | tf_op jit(solution)/shard_map/reshape | solution.py:81
  485.2 10.8 %gather_fusion.2 = bf16[512,3584]{1,0:T(8,128)(2,1)} fusion(bf16[640,3584]{1,0:T(8,128)(2,1)} %reshape.180, s32[1024]{0:T(1024)S(1)} %pad_clamp_fusion), kind=kCustom, calls=%fused_computation.2 | custom fusion | bytes 7342080 | tf_op jit(solution)/shard_map/gather | solution.py:81
  496.0 7.0 %reshape.181 = bf16[128,4,3584]{2,1,0:T(4,128)(2,1)} reshape(bf16[512,3584]{1,0:T(8,128)(2,1)} %gather_fusion.2) | data formatting | bytes 7340032 | tf_op jit(solution)/shard_map/reshape | solution.py:83
  503.0 7.6 %broadcast_select_fusion.2 = (bf16[128,4,3584]{2,0,1:T(8,128)(2,1)S(1)}, bf16[128,4,3584]{2,0,1:T(8,128)(2,1)S(1)}) fusion(pred[128,4]{0,1:T(4,128)(4,1)S(1)} %fusion.23, bf16[128,4,3584]{2,1,0:T(4,128)(2,1)} %reshape.181, bf16[128,4,3584]{2,1,0:T(4,128)(2,1)} %reshape.179), kind=kLoop, calls=%fused_computation.14 | loop fusion | flops 3670016 | bytes 14680576 | tf_op jit(solution)/shard_map/jit(_where)/select_n | solution.py:85
  510.6 2.5 fusion.7
  (53 shorter events, 5.2 us)
Async XLA Ops:
  0.6 6.2 %copy-start = (bf16[128,3584]{1,0:T(8,128)(2,1)S(1)}, bf16[128,3584]{1,0:T(8,128)(2,1)}, u32[]{:S(2)}) copy-start(bf16[128,3584]{1,0:T(8,128)(2,1)} %param.8) | copy-start | bytes 2752516
  123.0 4.5 copy-start.2
  123.0 4.8 copy-start.4
  127.4 29.7 %collective-permute-start = (bf16[128,5,3584]{2,0,1:T(8,128)(2,1)}, bf16[128,5,3584]{2,0,1:T(8,128)(2,1)}, u32[]{:S(2)}, u32[]{:S(2)}) collective-permute-start(bf16[128,5,3584]{2,0,1:T(8,128)(2,1)} %copy.55), channel_id=1, source_target_pairs={{0,1},{1,0},{2,3},{3,2},{4,5},{5,4},{6,7},{7,6},{8,9},{9,8},{10,11... | collective-permute-start | bytes 13762568 | tf_op jit(solution)/shard_map/ppermute | solution.py:16
  144.3 116.4 %all-to-all-start.4 = ((f32[64,28,128]{2,1,0:T(8,128)}), f32[64,28,128]{2,1,0:T(8,128)S(1)}, u32[]{:S(2)}, u32[]{:S(2)}) async-start(f32[64,28,128]{2,1,0:T(8,128)} %reshape.182), calls=%async_computation.4 | async-start | bytes 2097152 | tf_op jit(solution)/shard_map/all_to_all | solution.py:32
  188.5 13.7 %copy-start.3 = (bf16[1280,3584]{1,0:T(8,128)(2,1)S(1)}, bf16[1280,3584]{1,0:T(8,128)(2,1)}, u32[]{:S(2)}) copy-start(bf16[1280,3584]{1,0:T(8,128)(2,1)} %reshape.176) | copy-start | bytes 27525124
  188.5 27.3 %slice-start = ((s8[7340032]{0:T(1024)(128)(4,1)}), s8[4194304]{0:T(1024)(128)(4,1)S(1)}, s32[]{:S(2)}) async-start(s8[7340032]{0:T(1024)(128)(4,1)} %bitcast.95), calls=%async_computation.5 | async-start | bytes 8388608
  202.2 13.6 %slice-start.1 = ((s8[7340032]{0:T(1024)(128)(4,1)}), s8[3145728]{0:T(1024)(128)(4,1)S(1)}, s32[]{:S(2)}) async-start(s8[7340032]{0:T(1024)(128)(4,1)} %bitcast.95), calls=%async_computation.6 | async-start | bytes 6291456
  260.5 10.0 %collective-permute-start.1 = (bf16[128,5,3584]{2,0,1:T(8,128)(2,1)}, bf16[128,5,3584]{2,0,1:T(8,128)(2,1)}, u32[]{:S(2)}, u32[]{:S(2)}) collective-permute-start(bf16[128,5,3584]{2,0,1:T(8,128)(2,1)} %copy.57), channel_id=1, source_target_pairs={{0,1},{1,0},{2,3},{3,2},{4,5},{5,4},{6,7},{7,6},{8,9},{9,8},{10,11... | collective-permute-start | bytes 13762568 | tf_op jit(solution)/shard_map/ppermute | solution.py:16
  260.7 110.1 %all-to-all-start.1 = ((bf16[128,5,3584]{2,1,0:T(8,128)(2,1)}), bf16[128,5,3584]{2,1,0:T(8,128)(2,1)}, u32[]{:S(2)}, u32[]{:S(2)}) async-start(bf16[128,5,3584]{2,1,0:T(8,128)(2,1)} %get-tuple-element.4), calls=%async_computation.1 | async-start | bytes 14680064 | tf_op jit(solution)/shard_map/all_to_all | solution.py:77
  278.4 97.7 %copy-start.5 = (f32[128,8]{0,1:T(8,128)S(1)}, f32[128,8]{0,1:T(8,128)}, u32[]{:S(2)}) copy-start(f32[128,8]{0,1:T(8,128)} %param.11) | copy-start | bytes 12292
  370.7 106.4 %all-to-all-start.2 = ((bf16[128,5,3584]{2,1,0:T(8,128)(2,1)}), bf16[128,5,3584]{2,1,0:T(8,128)(2,1)}, u32[]{:S(2)}, u32[]{:S(2)}) async-start(bf16[128,5,3584]{2,1,0:T(8,128)(2,1)} %copy.58), calls=%async_computation.2 | async-start | bytes 14680064 | tf_op jit(solution)/shard_map/all_to_all | solution.py:78
  503.0 10.1 %copy-start.1 = (bf16[128,3584]{1,0:T(8,128)(2,1)S(1)}, bf16[128,3584]{1,0:T(8,128)(2,1)}, u32[]{:S(2)}) copy-start(bf16[128,3584]{1,0:T(8,128)(2,1)} %param.8) | copy-start | bytes 2752516
where the time goes:
time: 522 us; the launch traced here: 514 us
  waiting for transfers between devices  167 us (32%)
  local copies, waits for them, and re-layouts  130 us (25%)
  blocking collectives  114 us (22%)
  matrix products  43.6 us (8%)
  other arithmetic  29.6 us (6%)
  starting transfers between devices  28.3 us (5%)
    all_to_all x1, blocking collectives, body(): lax.all_to_all(pair_send, ('edp', 'ep'), split_axis=0, concat_axis=0, til...  99 us
    all_to_all x1, waiting for transfers between devices, body(): lax.all_to_all(own_out, ('edp', 'ep'), split_axis=0, concat_axis=0, tiled...  92.3 us
    all_to_all x1, waiting for transfers between devices, body(): lax.all_to_all(partner_out, ('edp', 'ep'), split_axis=0, concat_axis=0, t...  74.3 us
    dot_general x1, matrix products, body(): jnp.dot(hidden, w_down[0], preferred_element_type=jnp.float32)  16.3 us
    all_to_all x1, blocking collectives, sent_and_summed(): lax.all_to_all(parts, axis, split_axis=0, concat_axis=0, tiled=True)  15.2 us
    reshape x1, local copies, waits for them, and re-layouts, body(): row_block = received.reshape(-1, model_width)  14.6 us
    reshape x1, local copies, waits for them, and re-layouts, body(): both_out = result.reshape(in_shape)  14.2 us
    dot_general x1, matrix products, body(): up_act = jnp.dot(row_block, w_up[0], preferred_element_type=jnp.float32)  13.7 us
  transfers between devices with their start and end apart: 5, of which 2 were waited for; matrix products, arithmetic and copies ran while one was open for 27% of the time, Pallas kernels for 0%

commit v1 on v0

v1 whole, which is shorter than its diff:
```python
import functools

import jax
import jax.numpy as jnp
from jax import lax
from jax.experimental import pallas as pl
from jax.experimental.pallas import tpu as pltpu
from jax.sharding import PartitionSpec as P

MESH = pl.DeviceIdType.MESH
CHUNKS = 2
CHIPS = 64
PER = CHIPS // CHUNKS
CAP = 10
EXT = 128
TILE = 256
BF16 = jnp.bfloat16
F32 = jnp.float32


def place():
    edp = lax.axis_index("edp")
    ep = lax.axis_index("ep")
    return (ep // 8) % 4, (ep // 2) % 4, (ep // 32) * 2 + edp, ep % 2


def device(x, y, z, core):
    x, y, z = x % 4, y % 4, z % 4
    return {"edp": z % 2, "ep": (z // 2) * 32 + x * 8 + y * 2 + core}


def offset_of(chunk, q):
    many = 4 // CHUNKS
    dx, dy = q // (4 * many), (q // many) % 4
    dz = (q % many) * CHUNKS + (chunk + 8 - dx - dy) % CHUNKS
    return dx, dy, dz


def prep_body(pos, nodes, locals_, aff, tokens, send, hot, rows, sems):
    x, y, z = pos[0], pos[1], pos[2]
    count = tokens.shape[0]
    width = tokens.shape[1]
    slots = CHIPS * CAP
    affinity = aff[...]
    weight = 2.5 * affinity / jnp.sum(affinity, axis=1, keepdims=True)
    node, local = nodes[...], locals_[...]
    lane = lax.broadcasted_iota(jnp.int32, (count, 128), 1)
    many = 4 // CHUNKS
    offsets = []
    hit = jnp.zeros((count, 128), F32)
    for j in range(4):
        pair = node[:, j : j + 1] * 8 + (local[:, 2 * j : 2 * j + 1] >> 1)
        pz = ((pair >> 4) & 1) * 2 + (pair >> 5)
        dx = (((pair >> 2) & 3) - x + 4) & 3
        dy = ((pair & 3) - y + 4) & 3
        dz = (pz - z + 4) & 3
        chunk = (dx + dy + dz) & (CHUNKS - 1)
        off = chunk * PER + (dx * 4 + dy) * many + (dz // CHUNKS)
        offsets.append(off)
        hit = hit + (lane == off).astype(F32)
    row = lax.broadcasted_iota(jnp.int32, (count, count), 0)
    col = lax.broadcasted_iota(jnp.int32, (count, count), 1)
    earlier = (col < row).astype(F32).astype(BF16)
    before = jnp.dot(earlier, hit.astype(BF16), preferred_element_type=F32)
    slot_id = lax.broadcasted_iota(jnp.int32, (count, slots), 1)
    total = jnp.zeros((count, slots), F32)
    ext = jnp.zeros((slots, EXT), F32)
    dims = (((0,), (0,)), ((), ()))
    for j in range(4):
        rank = jnp.sum(jnp.where(lane == offsets[j], before, 0.0), axis=1, keepdims=True)
        slot = offsets[j] * CAP + rank.astype(jnp.int32)
        mine = (slot_id == slot).astype(F32)
        total = total + mine
        lead_even = (local[:, 2 * j : 2 * j + 1] & 1) == 0
        first, second = weight[:, 2 * j : 2 * j + 1], weight[:, 2 * j + 1 : 2 * j + 2]
        pieces = jnp.zeros((count, EXT), F32)
        for k, value in enumerate(
            (jnp.where(lead_even, first, second), jnp.where(lead_even, second, first))
        ):
            for part in range(3):
                piece = value.astype(BF16).astype(F32)
                pieces = jnp.where(lane == 3 * k + part, piece, pieces)
                value = value - piece
        ext = ext + lax.dot_general(
            mine.astype(BF16), pieces.astype(BF16), dims, preferred_element_type=F32
        )
    one_hot = total.astype(BF16)
    hot[...] = one_hot
    rows[:, width:] = ext.astype(BF16)
    part = width // 4
    for k in range(4):
        rows[:, k * part : (k + 1) * part] = lax.dot_general(
            one_hot, tokens[:, k * part : (k + 1) * part], dims, preferred_element_type=F32
        ).astype(BF16)
    copy = pltpu.make_async_copy(rows, send.reshape(slots, width + EXT), sems)
    copy.start()
    copy.wait()


def moe_body(
    send, w_gate, w_up, w_down, land, pair_out, back,
    gate_v, up_v, down_v, xs, hidden, theirs, mine, other, summed,
    w_sems, disp_send, disp_recv, local_sems, fwd_send, fwd_recv, x_sems,
    out_send, out_recv, p_sems, back_send, back_recv,
):
    x, y, z, core = place()
    width = w_gate.shape[1]
    half = PER * CAP
    partner = {"edp": lax.axis_index("edp"), "ep": lax.axis_index("ep") + 1 - 2 * core}

    loads = [
        pltpu.make_async_copy(w_gate.at[0], gate_v, w_sems.at[0]),
        pltpu.make_async_copy(w_up.at[0], up_v, w_sems.at[1]),
        pltpu.make_async_copy(w_down.at[0], down_v, w_sems.at[2]),
    ]
    for load in loads:
        load.start()

    barrier = pltpu.get_barrier_semaphore()

    def greet(n, carry):
        pl.semaphore_signal(
            barrier, 1, device_id=device(x + n // 16, y + n // 4, z + n, core), device_id_type=MESH
        )
        return carry

    lax.fori_loop(1, CHIPS, greet, 0)
    pl.semaphore_signal(barrier, 1, device_id=partner, device_id_type=MESH)
    pl.semaphore_wait(barrier, CHIPS)

    own = pltpu.make_async_copy(send.at[0, 0], land.at[0, 0], local_sems.at[0])
    own.start()

    def dispatch(chunk, first):
        def step(q, carry):
            dx, dy, dz = offset_of(chunk, q)
            pltpu.make_async_remote_copy(
                send.at[chunk, q], land.at[chunk, q], disp_send.at[chunk], disp_recv.at[chunk],
                device_id=device(x + dx, y + dy, z + dz, core), device_id_type=MESH,
            ).start()
            return carry

        lax.fori_loop(first, PER, step, 0)

    for chunk in range(CHUNKS):
        dispatch(chunk, 1 if chunk == 0 else 0)

    def many(ref, sem):
        return pltpu.make_async_copy(ref, ref, sem)

    forwards, swaps = [], []
    for chunk in range(CHUNKS):
        first = 1 if chunk == 0 else 0
        if chunk == 0:
            own.wait()
        got = land.at[chunk, pl.ds(first, PER - first)]
        many(got, disp_recv.at[chunk]).wait()
        rows_in = land.at[chunk].reshape(half, width + EXT)
        take = pltpu.make_async_copy(rows_in, xs.at[chunk, pl.ds(0, half)], x_sems.at[chunk])
        take.start()
        forward = pltpu.make_async_remote_copy(
            rows_in, xs.at[chunk, pl.ds(half, half)], fwd_send.at[chunk], fwd_recv.at[chunk],
            device_id=partner, device_id_type=MESH,
        )
        forward.start()
        forwards.append(forward)
        if chunk == 0:
            loads[0].wait()
            loads[1].wait()
        take.wait()
        forward.wait_recv()

        def gate_step(n, carry):
            cols = pl.ds(pl.multiple_of(n * TILE, TILE), TILE)
            block = xs[chunk, :, :width]
            gate = jnp.dot(block, gate_v[:, cols], preferred_element_type=F32)
            up = jnp.dot(block, up_v[:, cols], preferred_element_type=F32)
            hidden[:, cols] = (gate / (1.0 + jnp.exp(-gate)) * up).astype(BF16)
            return carry

        lax.fori_loop(0, w_gate.shape[2] // TILE, gate_step, 0)
        if chunk == 0:
            loads[2].wait()

        def down_to(dest, start):
            def down_step(n, carry):
                cols = pl.ds(pl.multiple_of(n * TILE, TILE), TILE)
                dest[:, cols] = jnp.dot(
                    hidden[start : start + half, :], down_v[:, cols], preferred_element_type=F32
                ).astype(BF16)
                return carry

            lax.fori_loop(0, width // TILE, down_step, 0)

        down_to(theirs.at[chunk], half)
        swap = pltpu.make_async_remote_copy(
            theirs.at[chunk], other.at[chunk], out_send.at[chunk], out_recv.at[chunk],
            device_id=partner, device_id_type=MESH,
        )
        swap.start()
        swaps.append(swap)
        down_to(mine, 0)
        ext = xs[chunk, :half, width:].astype(F32)
        lane = lax.broadcasted_iota(jnp.int32, ext.shape, 1)
        even = jnp.sum(jnp.where(lane < 3, ext, 0.0), axis=1, keepdims=True)
        odd = jnp.sum(jnp.where(lane < 3, 0.0, ext), axis=1, keepdims=True)
        is_even = (jnp.zeros_like(even).astype(jnp.int32) + core) == 0
        w_mine = jnp.where(is_even, even, odd)
        w_other = jnp.where(is_even, odd, even)
        swap.wait_recv()

        def sum_step(n, carry):
            cols = pl.ds(pl.multiple_of(n * TILE, TILE), TILE)
            summed[chunk, :, cols] = (
                w_mine * mine[:, cols].astype(F32) + w_other * other[chunk, :, cols].astype(F32)
            ).astype(BF16)
            return carry

        lax.fori_loop(0, width // TILE, sum_step, 0)
        put = pltpu.make_async_copy(
            summed.at[chunk], pair_out.at[chunk].reshape(half, width), p_sems.at[chunk]
        )
        put.start()
        put.wait()

        def home(q, carry):
            dx, dy, dz = offset_of(chunk, q)
            pltpu.make_async_remote_copy(
                pair_out.at[chunk, q], back.at[chunk, q], back_send.at[chunk], back_recv.at[chunk],
                device_id=device(x + 4 - dx, y + 4 - dy, z + 4 - dz, core), device_id_type=MESH,
            ).start()
            return carry

        lax.fori_loop(first, PER, home, 0)
        if chunk == 0:
            keep = pltpu.make_async_copy(pair_out.at[0, 0], back.at[0, 0], local_sems.at[1])
            keep.start()

    keep.wait()
    for chunk in range(CHUNKS):
        first = 1 if chunk == 0 else 0
        forwards[chunk].wait_send()
        swaps[chunk].wait_send()
        many(send.at[chunk, pl.ds(first, PER - first)], disp_send.at[chunk]).wait()
        many(pair_out.at[chunk, pl.ds(first, PER - first)], back_send.at[chunk]).wait()
        many(back.at[chunk, pl.ds(first, PER - first)], back_recv.at[chunk]).wait()


def mix_body(hot, back, out, rows, sems):
    half = PER * CAP
    copies = []
    for chunk in range(CHUNKS):
        copies.append(
            pltpu.make_async_copy(
                back.at[chunk].reshape(half, out.shape[1]), rows.at[pl.ds(chunk * half, half)],
                sems.at[chunk],
            )
        )
        copies[-1].start()
    for copy in copies:
        copy.wait()
    part = out.shape[1] // 4
    for k in range(4):
        cols = slice(k * part, (k + 1) * part)
        out[:, cols] = jnp.dot(
            hot[...], rows[:, cols], preferred_element_type=F32
        ).astype(out.dtype)


def body(tokens, node_ids, local_ids, affinity, w_gate, w_up, w_down, grad_parts):
    count, width = tokens.shape
    inner = w_gate.shape[2]
    half = PER * CAP
    slots = CHIPS * CAP
    vmem = pl.BlockSpec(memory_space=pltpu.VMEM)
    hbm = pl.BlockSpec(memory_space=pltpu.HBM)
    smem = pl.BlockSpec(memory_space=pltpu.SMEM)
    x, y, z, _ = place()
    pos = jnp.stack([x, y, z]).astype(jnp.int32)
    send, hot = pl.pallas_call(
        prep_body,
        name="prep",
        out_shape=(
            jax.ShapeDtypeStruct((CHUNKS, PER, CAP // 2, 2, width + EXT), BF16),
            jax.ShapeDtypeStruct((count, slots), BF16),
        ),
        in_specs=[smem, vmem, vmem, vmem, vmem],
        out_specs=(hbm, vmem),
        scratch_shapes=[
            pltpu.VMEM((slots, width + EXT), BF16),
            pltpu.SemaphoreType.DMA,
        ],
        compiler_params=pltpu.CompilerParams(vmem_limit_bytes=60 << 20),
    )(pos, node_ids, local_ids, affinity, tokens)

    dma = pltpu.SemaphoreType.DMA
    _, _, back = pl.pallas_call(
        moe_body,
        name="moe",
        out_shape=(
            jax.ShapeDtypeStruct((CHUNKS, PER, CAP // 2, 2, width + EXT), BF16),
            jax.ShapeDtypeStruct((CHUNKS, PER, CAP // 2, 2, width), BF16),
            jax.ShapeDtypeStruct((CHUNKS, PER, CAP // 2, 2, width), BF16),
        ),
        in_specs=[hbm] * 4,
        out_specs=(hbm,) * 3,
        scratch_shapes=[
            pltpu.VMEM((width, inner), BF16),
            pltpu.VMEM((width, inner), BF16),
            pltpu.VMEM((inner, width), BF16),
            pltpu.VMEM((CHUNKS, 2 * half, width + EXT), BF16),
            pltpu.VMEM((2 * half, inner), BF16),
            pltpu.VMEM((CHUNKS, half, width), BF16),
            pltpu.VMEM((half, width), BF16),
            pltpu.VMEM((CHUNKS, half, width), BF16),
            pltpu.VMEM((CHUNKS, half, width), BF16),
            dma((3,)),
            dma((CHUNKS,)), dma((CHUNKS,)), dma((2,)), dma((CHUNKS,)), dma((CHUNKS,)),
            dma((CHUNKS,)), dma((CHUNKS,)), dma((CHUNKS,)), dma((CHUNKS,)), dma((CHUNKS,)),
            dma((CHUNKS,)),
        ],
        compiler_params=pltpu.CompilerParams(
            collective_id=0, has_side_effects=True, vmem_limit_bytes=67043328
        ),
        cost_estimate=pl.CostEstimate(
            flops=6 * 2 * slots * width * inner, bytes_accessed=50 << 20, transcendentals=0
        ),
    )(send, w_gate, w_up, w_down)
    mixed = pl.pallas_call(
        mix_body,
        name="mix",
        out_shape=jax.ShapeDtypeStruct((count, width), BF16),
        in_specs=[vmem, hbm],
        out_specs=vmem,
        scratch_shapes=[pltpu.VMEM((slots, width), BF16), dma((CHUNKS,))],
        compiler_params=pltpu.CompilerParams(vmem_limit_bytes=60 << 20),
    )(hot, back)
    router_grad = lax.psum_scatter(
        grad_parts[0], ("edp", "ep"), scatter_dimension=0, tiled=True
    )
    return mixed, router_grad


def solution(mesh):
    spec2 = P(("edp", "ep"), None)
    spec3 = P(("edp", "ep"), None, None)
    return jax.shard_map(
        body,
        mesh=mesh,
        in_specs=(spec2,) * 4 + (spec3,) * 4,
        out_specs=(spec2, spec2),
        check_vma=False,
    )
```

time: 522 us -> 591 us (1.13)
  the two profiles are of different devices: /device:TPU:10 before, /device:TPU:42 now
where the time goes in v1:
time: 591 us; the launch traced here: 588 us
  blocking collectives  264 us (45%)
  Pallas kernels  186 us (31%)
  starting transfers between devices  117 us (20%)
  local copies, waits for them, and re-layouts  18.8 us (3%)
    unnamed x1, blocking collectives  264 us
    pallas_call x1, Pallas kernels, body(): pl.pallas_call(moe_body, name='moe', out_shape=(jax.ShapeDtypeStruct((CHU...  174 us
    unnamed x16, starting transfers between devices  117 us
    unnamed x6, local copies, waits for them, and re-layouts  18.8 us
  transfers between devices with their start and end apart: 16, of which 0 were waited for; matrix products, arithmetic and copies ran while one was open for 1% of the time, Pallas kernels for 32%

profile of v1, /device:TPU:42, one launch (start us, length us, event | category | flops | bytes accessed | tf_op | source)
XLA Modules:
  0.0 588.0 jit_solution(10333900571420053034)
XLA Ops:
  0.6 263.7 %fusion = f32[32,128]{1,0:T(8,128)} fusion(f32[3584,128]{1,0:T(8,128)} %bitcast.4), kind=kCustom, calls=%all-reduce-scatter | all-reduce-scatter fusion | flops 524289 | bytes 1851392
  264.3 0.7 slice
  265.0 56.1 %collective-permute-start.15 = (f32[28,128]{1,0:T(8,128)S(1)}, f32[28,128]{1,0:T(8,128)}, u32[]{:S(2)}, u32[]{:S(2)}) collective-permute-start(f32[28,128]{1,0:T(8,128)S(1)} %slice), channel_id=1, source_target_pairs={{0,16},{1,17},{2,18},{3,19},{4,20},{5,21},{6,22},{7,23},{8,24},{9,... | collective-permute-start | bytes 43016
  321.1 1.9 collective-permute-start.14
  323.0 2.9 collective-permute-start.13
  325.9 8.0 %collective-permute-start.12 = (f32[32,128]{1,0:T(8,128)}, f32[32,128]{1,0:T(8,128)}, u32[]{:S(2)}, u32[]{:S(2)}) collective-permute-start(f32[32,128]{1,0:T(8,128)} %fusion), channel_id=1, source_target_pairs={{0,13},{1,14},{2,15},{3,16},{4,17},{5,18},{6,19},{7,20},{8,21},{9,... | collective-permute-start | bytes 49160
  333.9 10.3 %collective-permute-start.11 = (f32[32,128]{1,0:T(8,128)}, f32[32,128]{1,0:T(8,128)}, u32[]{:S(2)}, u32[]{:S(2)}) collective-permute-start(f32[32,128]{1,0:T(8,128)} %fusion), channel_id=1, source_target_pairs={{0,12},{1,13},{2,14},{3,15},{4,16},{5,17},{6,18},{7,19},{8,20},{9,... | collective-permute-start | bytes 49160
  344.2 7.7 %collective-permute-start.10 = (f32[32,128]{1,0:T(8,128)}, f32[32,128]{1,0:T(8,128)}, u32[]{:S(2)}, u32[]{:S(2)}) collective-permute-start(f32[32,128]{1,0:T(8,128)} %fusion), channel_id=1, source_target_pairs={{0,11},{1,12},{2,13},{3,14},{4,15},{5,16},{6,17},{7,18},{8,19},{9,... | collective-permute-start | bytes 49160
  352.0 0.0 collective-permute-done.14
  352.0 6.6 %collective-permute-start.9 = (f32[32,128]{1,0:T(8,128)}, f32[32,128]{1,0:T(8,128)}, u32[]{:S(2)}, u32[]{:S(2)}) collective-permute-start(f32[32,128]{1,0:T(8,128)} %fusion), channel_id=1, source_target_pairs={{0,10},{1,11},{2,12},{3,13},{4,14},{5,15},{6,16},{7,17},{8,18},{9,... | collective-permute-start | bytes 49160
  358.6 0.0 collective-permute-done.13
  358.6 1.9 collective-permute-start.8
  360.6 0.0 collective-permute-done.12
  360.6 1.9 collective-permute-start.7
  362.5 1.9 collective-permute-start.6
  364.4 0.0 collective-permute-done.10
  364.4 4.4 collective-permute-start.5
  368.9 0.7 pad_add_fusion.pos
  369.5 1.4 copy.13.nodes
  370.9 1.4 copy.14.locals_
  372.3 1.4 copy.15.aff
  373.7 6.8 %prep.1 = (bf16[2,32,5,2,3712]{4,3,2,1,0:T(2,128)(2,1)}, bf16[128,640]{1,0:T(8,128)(2,1)}) custom-call(s32[3]{0:T(128)} %pad_add_fusion.pos, s32[128,4]{1,0:T(8,128)} %copy.13.nodes, s32[128,8]{1,0:T(8,128)} %copy.14.locals_, f32[128,8]{1,0:T(8,128)} %copy.15.aff, bf16[128,3584]{1,0:T(8,128)(2,1)} %tokens.1), custom_call_target="tpu_custom_call" | custom-call | tf_op jit(solution)/shard_map/prep/pallas_call | solution.py:280
  380.6 0.0 collective-permute-done.9
  380.6 1.9 collective-permute-start.4
  382.5 4.6 collective-permute-start.3
  387.1 1.9 collective-permute-start.2
  389.1 2.2 collective-permute-start.1
  391.3 3.2 collective-permute-start
  394.5 174.4 %moe.1 = (bf16[2,32,5,2,3712]{4,3,2,1,0:T(2,128)(2,1)}, bf16[2,32,5,2,3584]{4,3,2,1,0:T(2,128)(2,1)}, bf16[2,32,5,2,3584]{4,3,2,1,0:T(2,128)(2,1)}) custom-call(bf16[2,32,5,2,3712]{4,3,2,1,0:T(2,128)(2,1)} %get-tuple-element.6.send, bf16[1,3584,1024]{2,1,0:T(8,128)(2,1)} %w_gate.1, bf16[1,3584,1024]{2,1,0:T(8,128)(2,1)} %w_up.1, bf16[1,1024,3584]{2,1,0:T(8,128)(2,1)} %w_down.1), custom_call_target="tpu_custom_call" | custom-call | flops 28185722880 | bytes 52428800 | tf_op jit(solution)/shard_map/moe/pallas_call | solution.py:297
  568.9 5.2 mix.1
  574.1 13.3 %concatenate = f32[540,128]{1,0:T(8,128)S(1)} concatenate(f32[28,128]{1,0:T(8,128)} %collective-permute-done.15, f32[32,128]{1,0:T(8,128)} %collective-permute-done.14, f32[32,128]{1,0:T(8,128)} %collective-permute-done.13, f32[32,128]{1,0:T(8,128)} %collective-permute-done.12, f32[32,128]{1,0:T(8,128)} %collective-permute-done.11, f32[32,128]{1,0:T(8,128)} %collective-permute-done.10, ...), dimensions={0} | concatenate | bytes 552960
  587.4 0.6 constant_dynamic-slice_fusion
  (11 shorter events, 0.0 us)
Async XLA Ops:
  265.0 79.2 %collective-permute-start.15 = (f32[28,128]{1,0:T(8,128)S(1)}, f32[28,128]{1,0:T(8,128)}, u32[]{:S(2)}, u32[]{:S(2)}) collective-permute-start(f32[28,128]{1,0:T(8,128)S(1)} %slice), channel_id=1, source_target_pairs={{0,16},{1,17},{2,18},{3,19},{4,20},{5,21},{6,22},{7,23},{8,24},{9,... | collective-permute-start | bytes 43016
  321.1 30.9 %collective-permute-start.14 = (f32[32,128]{1,0:T(8,128)}, f32[32,128]{1,0:T(8,128)}, u32[]{:S(2)}, u32[]{:S(2)}) collective-permute-start(f32[32,128]{1,0:T(8,128)} %fusion), channel_id=1, source_target_pairs={{0,15},{1,16},{2,17},{3,18},{4,19},{5,20},{6,21},{7,22},{8,23},{9,... | collective-permute-start | bytes 49160
  323.0 35.6 %collective-permute-start.13 = (f32[32,128]{1,0:T(8,128)}, f32[32,128]{1,0:T(8,128)}, u32[]{:S(2)}, u32[]{:S(2)}) collective-permute-start(f32[32,128]{1,0:T(8,128)} %fusion), channel_id=1, source_target_pairs={{0,14},{1,15},{2,16},{3,17},{4,18},{5,19},{6,20},{7,21},{8,22},{9,... | collective-permute-start | bytes 49160
  325.9 34.7 %collective-permute-start.12 = (f32[32,128]{1,0:T(8,128)}, f32[32,128]{1,0:T(8,128)}, u32[]{:S(2)}, u32[]{:S(2)}) collective-permute-start(f32[32,128]{1,0:T(8,128)} %fusion), channel_id=1, source_target_pairs={{0,13},{1,14},{2,15},{3,16},{4,17},{5,18},{6,19},{7,20},{8,21},{9,... | collective-permute-start | bytes 49160
  333.9 28.6 %collective-permute-start.11 = (f32[32,128]{1,0:T(8,128)}, f32[32,128]{1,0:T(8,128)}, u32[]{:S(2)}, u32[]{:S(2)}) collective-permute-start(f32[32,128]{1,0:T(8,128)} %fusion), channel_id=1, source_target_pairs={{0,12},{1,13},{2,14},{3,15},{4,16},{5,17},{6,18},{7,19},{8,20},{9,... | collective-permute-start | bytes 49160
  344.2 20.2 %collective-permute-start.10 = (f32[32,128]{1,0:T(8,128)}, f32[32,128]{1,0:T(8,128)}, u32[]{:S(2)}, u32[]{:S(2)}) collective-permute-start(f32[32,128]{1,0:T(8,128)} %fusion), channel_id=1, source_target_pairs={{0,11},{1,12},{2,13},{3,14},{4,15},{5,16},{6,17},{7,18},{8,19},{9,... | collective-permute-start | bytes 49160
  352.0 28.6 %collective-permute-start.9 = (f32[32,128]{1,0:T(8,128)}, f32[32,128]{1,0:T(8,128)}, u32[]{:S(2)}, u32[]{:S(2)}) collective-permute-start(f32[32,128]{1,0:T(8,128)} %fusion), channel_id=1, source_target_pairs={{0,10},{1,11},{2,12},{3,13},{4,14},{5,15},{6,16},{7,17},{8,18},{9,... | collective-permute-start | bytes 49160
  358.6 23.9 %collective-permute-start.8 = (f32[32,128]{1,0:T(8,128)}, f32[32,128]{1,0:T(8,128)}, u32[]{:S(2)}, u32[]{:S(2)}) collective-permute-start(f32[32,128]{1,0:T(8,128)} %fusion), channel_id=1, source_target_pairs={{0,9},{1,10},{2,11},{3,12},{4,13},{5,14},{6,15},{7,16},{8,17},{9,1... | collective-permute-start | bytes 49160
  360.6 26.6 %collective-permute-start.7 = (f32[32,128]{1,0:T(8,128)}, f32[32,128]{1,0:T(8,128)}, u32[]{:S(2)}, u32[]{:S(2)}) collective-permute-start(f32[32,128]{1,0:T(8,128)} %fusion), channel_id=1, source_target_pairs={{0,8},{1,9},{2,10},{3,11},{4,12},{5,13},{6,14},{7,15},{8,16},{9,17... | collective-permute-start | bytes 49160
  362.5 26.6 %collective-permute-start.6 = (f32[32,128]{1,0:T(8,128)}, f32[32,128]{1,0:T(8,128)}, u32[]{:S(2)}, u32[]{:S(2)}) collective-permute-start(f32[32,128]{1,0:T(8,128)} %fusion), channel_id=1, source_target_pairs={{0,7},{1,8},{2,9},{3,10},{4,11},{5,12},{6,13},{7,14},{8,15},{9,16}... | collective-permute-start | bytes 49160
  364.4 26.8 %collective-permute-start.5 = (f32[32,128]{1,0:T(8,128)}, f32[32,128]{1,0:T(8,128)}, u32[]{:S(2)}, u32[]{:S(2)}) collective-permute-start(f32[32,128]{1,0:T(8,128)} %fusion), channel_id=1, source_target_pairs={{0,6},{1,7},{2,8},{3,9},{4,10},{5,11},{6,12},{7,13},{8,14},{9,15},... | collective-permute-start | bytes 49160
  380.6 193.5 %collective-permute-start.4 = (f32[32,128]{1,0:T(8,128)}, f32[32,128]{1,0:T(8,128)}, u32[]{:S(2)}, u32[]{:S(2)}) collective-permute-start(f32[32,128]{1,0:T(8,128)} %fusion), channel_id=1, source_target_pairs={{0,5},{1,6},{2,7},{3,8},{4,9},{5,10},{6,11},{7,12},{8,13},{9,14},{... | collective-permute-start | bytes 49160
  382.5 191.6 %collective-permute-start.3 = (f32[32,128]{1,0:T(8,128)}, f32[32,128]{1,0:T(8,128)}, u32[]{:S(2)}, u32[]{:S(2)}) collective-permute-start(f32[32,128]{1,0:T(8,128)} %fusion), channel_id=1, source_target_pairs={{0,4},{1,5},{2,6},{3,7},{4,8},{5,9},{6,10},{7,11},{8,12},{9,13},{1... | collective-permute-start | bytes 49160
  387.1 187.0 %collective-permute-start.2 = (f32[32,128]{1,0:T(8,128)}, f32[32,128]{1,0:T(8,128)}, u32[]{:S(2)}, u32[]{:S(2)}) collective-permute-start(f32[32,128]{1,0:T(8,128)} %fusion), channel_id=1, source_target_pairs={{0,3},{1,4},{2,5},{3,6},{4,7},{5,8},{6,9},{7,10},{8,11},{9,12},{10... | collective-permute-start | bytes 49160
  389.1 185.0 %collective-permute-start.1 = (f32[32,128]{1,0:T(8,128)}, f32[32,128]{1,0:T(8,128)}, u32[]{:S(2)}, u32[]{:S(2)}) collective-permute-start(f32[32,128]{1,0:T(8,128)} %fusion), channel_id=1, source_target_pairs={{0,2},{1,3},{2,4},{3,5},{4,6},{5,7},{6,8},{7,9},{8,10},{9,11},{10,... | collective-permute-start | bytes 49160
  391.3 182.8 %collective-permute-start = (f32[32,128]{1,0:T(8,128)}, f32[32,128]{1,0:T(8,128)}, u32[]{:S(2)}, u32[]{:S(2)}) collective-permute-start(f32[32,128]{1,0:T(8,128)} %fusion), channel_id=1, source_target_pairs={{0,1},{1,2},{2,3},{3,4},{4,5},{5,6},{6,7},{7,8},{8,9},{9,10},{10,1... | collective-permute-start | bytes 49160

commit v2 on v1

v2 whole, which is shorter than its diff:
```python
import jax
import jax.numpy as jnp
from jax import lax
from jax.experimental import pallas as pl
from jax.experimental.pallas import tpu as pltpu
from jax.sharding import PartitionSpec as P

MESH = pl.DeviceIdType.MESH
CHUNKS = 2
CHIPS = 64
PER = CHIPS // CHUNKS
CAP = 10
HALF = PER * CAP
PAIRS = CAP // 2
EXT = 128
TILE = 256
BF16 = jnp.bfloat16
F32 = jnp.float32
I32 = jnp.int32
TURN = (((0,), (0,)), ((), ()))
SIDE = (((1,), (1,)), ((), ()))


def place():
    edp = lax.axis_index("edp")
    ep = lax.axis_index("ep")
    return (ep // 8) % 4, (ep // 2) % 4, (ep // 32) * 2 + edp, ep % 2


def device(x, y, z, core):
    x, y, z = x % 4, y % 4, z % 4
    return {"edp": z % 2, "ep": (z // 2) * 32 + x * 8 + y * 2 + core}


def slot_of(dx, dy, dz):
    return (dx + dy + dz) % CHUNKS, (dx * 4 + dy) * (4 // CHUNKS) + dz // CHUNKS


def send_order():
    far = sorted(
        ((x, y, z) for x in range(4) for y in range(4) for z in range(4)),
        key=lambda o: -sum(min(d, 4 - d) for d in o),
    )
    order = []
    for o in far:
        for k in range(3):
            for s in (1, -1):
                other = tuple(s * o[(i + k) % 3] % 4 for i in range(3))
                if other not in order and any(other):
                    order.append(other)
    return [[o for o in order if slot_of(*o)[0] == chunk] for chunk in range(CHUNKS)]


ORDER = send_order()


def many(ref, sem):
    return pltpu.make_async_copy(ref, ref, sem)


def tile_at(n):
    return pl.ds(pl.multiple_of(n * TILE, TILE), TILE)


def moe_body(
    nodes, locals_, aff, tokens, w_gate, w_up, w_down, grads,
    mixed, router, send, land, pair_out, back,
    node_v, local_v, aff_v, tok_v, gate_v, up_v, down_v, hot, rows, xs, hidden, theirs, mine,
    other, acc, g_mine, g_other, g_sum, g_in, g_tot,
    in_sems, w_sems, row_sems, disp_send, disp_recv, own_sems, fwd_send, fwd_recv, x_sems,
    out_send, out_recv, p_sems, back_send, back_recv, mix_sems,
    g_load, g_swap_send, g_swap_recv, g_send, g_recv, g_out, g_out_send, g_out_recv,
):
    x, y, z, core = place()
    z_lo = lax.axis_index("edp")
    width = tokens.shape[1]
    count = tokens.shape[0]
    partner = {"edp": lax.axis_index("edp"), "ep": lax.axis_index("ep") + 1 - 2 * core}

    small = [
        pltpu.make_async_copy(src, dst, in_sems.at[n])
        for n, (src, dst) in enumerate(
            ((nodes, node_v), (locals_, local_v), (aff, aff_v), (tokens, tok_v))
        )
    ]
    for load in small:
        load.start()
    barrier = pltpu.get_barrier_semaphore()

    def greet(n, carry):
        pl.semaphore_signal(
            barrier, 1, device_id=device(x + n // 16, y + n // 4, z + n, core), device_id_type=MESH
        )
        return carry

    lax.fori_loop(1, CHIPS, greet, 0)
    pl.semaphore_signal(barrier, 1, device_id=partner, device_id_type=MESH)
    g_take = pltpu.make_async_copy(grads.at[core], g_mine, g_load)
    g_take.start()
    loads = [
        pltpu.make_async_copy(w_gate.at[0], gate_v, w_sems.at[0]),
        pltpu.make_async_copy(w_up.at[0], up_v, w_sems.at[1]),
        pltpu.make_async_copy(w_down.at[0], down_v, w_sems.at[2]),
    ]
    for load in loads:
        load.start()
    for load in small:
        load.wait()

    affinity = aff_v[...]
    weight = 2.5 * affinity / jnp.sum(affinity, axis=0, keepdims=True)
    node, local = node_v[...], local_v[...]
    chip_id = lax.broadcasted_iota(I32, (CHIPS, count), 0)
    offsets = []
    hit = jnp.zeros((CHIPS, count), F32)
    for j in range(4):
        pair = node[j : j + 1, :] * 8 + (local[2 * j : 2 * j + 1, :] >> 1)
        pz = ((pair >> 4) & 1) * 2 + (pair >> 5)
        dx = (((pair >> 2) & 3) - x + 4) & 3
        dy = ((pair & 3) - y + 4) & 3
        dz = (pz - z + 4) & 3
        chunk = (dx + dy + dz) & (CHUNKS - 1)
        off = chunk * PER + (dx * 4 + dy) * (4 // CHUNKS) + dz // CHUNKS
        offsets.append(off)
        hit = hit + (chip_id == off).astype(F32)
    row = lax.broadcasted_iota(I32, (count, count), 0)
    col = lax.broadcasted_iota(I32, (count, count), 1)
    earlier = (row < col).astype(F32).astype(BF16)
    before = jnp.dot(hit.astype(BF16), earlier, preferred_element_type=F32)
    slots, pieces = [], []
    for j in range(4):
        rank = jnp.sum(jnp.where(chip_id == offsets[j], before, 0.0), axis=0, keepdims=True)
        slots.append(offsets[j] * CAP + rank.astype(I32))
        lead_even = (local[2 * j : 2 * j + 1, :] & 1) == 0
        first, second = weight[2 * j : 2 * j + 1, :], weight[2 * j + 1 : 2 * j + 2, :]
        parts = jnp.zeros((EXT, count), F32)
        for k, value in enumerate(
            (jnp.where(lead_even, first, second), jnp.where(lead_even, second, first))
        ):
            for part in range(3):
                piece = value.astype(BF16).astype(F32)
                parts = jnp.where(row == 3 * k + part, piece, parts)
                value = value - piece
        pieces.append(parts.astype(BF16))

    def fill(chunk):
        slot_id = lax.broadcasted_iota(I32, (HALF, count), 0) + chunk * HALF
        total = jnp.zeros((HALF, count), F32)
        ext = jnp.zeros((HALF, EXT), F32)
        for j in range(4):
            match = (slot_id == slots[j]).astype(F32)
            total = total + match
            ext = ext + lax.dot_general(
                match.astype(BF16), pieces[j], SIDE, preferred_element_type=F32
            )
        one_hot = total.astype(BF16)
        hot[chunk] = one_hot
        rows[chunk, :, width:] = ext.astype(BF16)
        part = width // 4
        for k in range(4):
            rows[chunk, :, k * part : (k + 1) * part] = jnp.dot(
                one_hot, tok_v[:, k * part : (k + 1) * part], preferred_element_type=F32
            ).astype(BF16)
        copy = pltpu.make_async_copy(
            rows.at[chunk], send.at[chunk].reshape(HALF, width + EXT), row_sems.at[chunk]
        )
        copy.start()
        return copy

    def dispatch(chunk):
        def step(p, carry):
            for o in ORDER[chunk]:
                q = slot_of(*o)[1]
                pltpu.make_async_remote_copy(
                    send.at[chunk, q, p], land.at[chunk, q, p],
                    disp_send.at[chunk], disp_recv.at[chunk],
                    device_id=device(x + o[0], y + o[1], z + o[2], core), device_id_type=MESH,
                ).start()
            return carry

        lax.fori_loop(0, PAIRS, step, 0)

    filled = fill(0)
    pl.semaphore_wait(barrier, CHIPS)
    g_swap = pltpu.make_async_remote_copy(
        grads.at[1 - core], g_other, g_swap_send, g_swap_recv,
        device_id=partner, device_id_type=MESH,
    )
    g_swap.start()
    filled.wait()
    own = pltpu.make_async_copy(send.at[0, 0], land.at[0, 0], own_sems.at[0])
    own.start()
    dispatch(0)
    for chunk in range(1, CHUNKS):
        fill(chunk).wait()
        dispatch(chunk)

    blocks = g_sum.shape[0]
    home_chip = z * 16 + x * 4 + y
    holder = z_lo == core
    g_take.wait()
    g_swap.wait_recv()

    def g_add(k, carry):
        g_sum[k] = (g_mine[k] + g_other[k]).astype(BF16)
        return carry

    lax.fori_loop(0, blocks, g_add, 0)

    def g_push(k, carry):
        tz, tx, ty = (k // 16) * 2 + core, (k // 4) % 4, k % 4
        here = (tz == z) & (tx == x) & (ty == y)

        @pl.when(here)
        def _():
            g_in[home_chip] = g_sum[k]

        @pl.when(jnp.logical_not(here))
        def _():
            pltpu.make_async_remote_copy(
                g_sum.at[k], g_in.at[home_chip], g_send, g_recv,
                device_id=device(tx, ty, tz, core), device_id_type=MESH,
            ).start()

        return carry

    lax.fori_loop(0, blocks, g_push, 0)

    forwards, swaps = [], []
    keep = None
    for chunk in range(CHUNKS):
        first = 1 if chunk == 0 else 0
        if chunk == 0:
            own.wait()
        many(land.at[chunk, pl.ds(first, PER - first)], disp_recv.at[chunk]).wait()
        rows_in = land.at[chunk].reshape(HALF, width + EXT)
        forward = pltpu.make_async_remote_copy(
            rows_in, xs.at[chunk, pl.ds(HALF, HALF)], fwd_send.at[chunk], fwd_recv.at[chunk],
            device_id=partner, device_id_type=MESH,
        )
        forward.start()
        forwards.append(forward)
        take = pltpu.make_async_copy(rows_in, xs.at[chunk, pl.ds(0, HALF)], x_sems.at[chunk])
        take.start()
        if chunk == 0:
            loads[0].wait()
            loads[1].wait()
        take.wait()
        forward.wait_recv()

        def gate_step(n, carry):
            cols = tile_at(n)
            block = xs[chunk, :, :width]
            gate = jnp.dot(block, gate_v[:, cols], preferred_element_type=F32)
            up = jnp.dot(block, up_v[:, cols], preferred_element_type=F32)
            hidden[:, cols] = (gate / (1.0 + jnp.exp(-gate)) * up).astype(BF16)
            return carry

        lax.fori_loop(0, gate_v.shape[1] // TILE, gate_step, 0)
        if chunk == 0:
            loads[2].wait()

        def their_step(n, carry):
            cols = tile_at(n)
            theirs[chunk, :, cols] = jnp.dot(
                hidden[HALF:, :], down_v[:, cols], preferred_element_type=F32
            ).astype(BF16)
            return carry

        lax.fori_loop(0, width // TILE, their_step, 0)
        swap = pltpu.make_async_remote_copy(
            theirs.at[chunk], other.at[chunk], out_send.at[chunk], out_recv.at[chunk],
            device_id=partner, device_id_type=MESH,
        )
        swap.start()
        swaps.append(swap)

        def mine_step(n, carry):
            cols = tile_at(n)
            mine[:, cols] = jnp.dot(
                hidden[:HALF, :], down_v[:, cols], preferred_element_type=F32
            ).astype(BF16)
            return carry

        lax.fori_loop(0, width // TILE, mine_step, 0)
        ext = xs[chunk, :HALF, width:].astype(F32)
        lane = lax.broadcasted_iota(I32, ext.shape, 1)
        even = jnp.sum(jnp.where(lane < 3, ext, 0.0), axis=1, keepdims=True)
        odd = jnp.sum(jnp.where(lane < 3, 0.0, ext), axis=1, keepdims=True)
        is_even = (lax.broadcasted_iota(I32, even.shape, 0) * 0 + core) == 0
        w_mine = jnp.where(is_even, even, odd)
        w_other = jnp.where(is_even, odd, even)
        swap.wait_recv()

        def sum_step(n, carry):
            cols = tile_at(n)
            rows[chunk, :, cols] = (
                w_mine * mine[:, cols].astype(F32) + w_other * other[chunk, :, cols].astype(F32)
            ).astype(BF16)
            return carry

        lax.fori_loop(0, width // TILE, sum_step, 0)
        put = pltpu.make_async_copy(
            rows.at[chunk, :, pl.ds(0, width)], pair_out.at[chunk].reshape(HALF, width),
            p_sems.at[chunk],
        )
        put.start()
        put.wait()

        def home(p, carry):
            for o in ORDER[chunk]:
                q = slot_of(*o)[1]
                pltpu.make_async_remote_copy(
                    pair_out.at[chunk, q, p], back.at[chunk, q, p],
                    back_send.at[chunk], back_recv.at[chunk],
                    device_id=device(x + 4 - o[0], y + 4 - o[1], z + 4 - o[2], core),
                    device_id_type=MESH,
                ).start()
            return carry

        lax.fori_loop(0, PAIRS, home, 0)
        if chunk == 0:
            keep = pltpu.make_async_copy(pair_out.at[0, 0], back.at[0, 0], own_sems.at[1])
            keep.start()

    @pl.when(holder)
    def _():
        many(g_in.at[pl.ds(0, CHIPS - 1)], g_recv).wait()

        def g_fold(s, total):
            return total + g_in[s].astype(F32)

        g_tot[...] = lax.fori_loop(0, CHIPS, g_fold, jnp.zeros(g_tot.shape, F32))

        def g_give(k, carry):
            at = pl.multiple_of(k * 4, 4)
            pltpu.make_async_copy(
                g_tot.at[pl.ds(pl.multiple_of(core * 28 + k * 4, 4), 4)], router.at[pl.ds(at, 4)],
                g_out,
            ).start()
            pltpu.make_async_remote_copy(
                g_tot.at[pl.ds(pl.multiple_of((1 - core) * 28 + k * 4, 4), 4)],
                router.at[pl.ds(at, 4)], g_out_send, g_out_recv,
                device_id=partner, device_id_type=MESH,
            ).start()
            return carry

        lax.fori_loop(0, 7, g_give, 0)

    keep.wait()
    for chunk in range(CHUNKS):
        first = 1 if chunk == 0 else 0
        many(back.at[chunk, pl.ds(first, PER - first)], back_recv.at[chunk]).wait()
        fetch = pltpu.make_async_copy(
            back.at[chunk].reshape(HALF, width), xs.at[chunk, pl.ds(0, HALF), pl.ds(0, width)],
            mix_sems.at[chunk],
        )
        fetch.start()
        fetch.wait()
        part = width // 4
        for k in range(4):
            cols = slice(k * part, (k + 1) * part)
            value = lax.dot_general(
                hot[chunk], xs[chunk, :HALF, cols], TURN, preferred_element_type=F32
            )
            if chunk:
                value = acc[:, cols] + value
            if chunk == CHUNKS - 1:
                mixed[:, cols] = value.astype(BF16)
            else:
                acc[:, cols] = value

    g_swap.wait_send()
    many(g_sum.at[pl.ds(0, blocks - 1)], g_send).wait()

    @pl.when(holder)
    def _():
        many(g_sum.at[0], g_out).wait()
        many(g_sum.at[0], g_out_send).wait()

    @pl.when(jnp.logical_not(holder))
    def _():
        many(g_sum.at[0], g_send).wait()
        many(g_sum.at[0], g_out_recv).wait()

    for chunk in range(CHUNKS):
        first = 1 if chunk == 0 else 0
        forwards[chunk].wait_send()
        swaps[chunk].wait_send()
        many(send.at[chunk, pl.ds(first, PER - first)], disp_send.at[chunk]).wait()
        many(pair_out.at[chunk, pl.ds(first, PER - first)], back_send.at[chunk]).wait()


def body(tokens, node_ids, local_ids, affinity, w_gate, w_up, w_down, grad_parts):
    count, width = tokens.shape
    inner = w_gate.shape[2]
    vmem = pl.BlockSpec(memory_space=pltpu.VMEM)
    hbm = pl.BlockSpec(memory_space=pltpu.HBM)
    dma = pltpu.SemaphoreType.DMA
    per_chunk = dma((CHUNKS,))
    blocks = CHIPS // 2
    deep = grad_parts.shape[1] // CHIPS
    lanes = grad_parts.shape[2]
    wide = jax.ShapeDtypeStruct((CHUNKS, PER, PAIRS, 2, width + EXT), BF16)
    plain = jax.ShapeDtypeStruct((CHUNKS, PER, PAIRS, 2, width), BF16)
    outs = pl.pallas_call(
        moe_body,
        name="moe",
        out_shape=(
            jax.ShapeDtypeStruct((count, width), BF16),
            jax.ShapeDtypeStruct((deep // 2, lanes), F32),
            wide, wide, plain, plain,
        ),
        in_specs=[hbm] * 8,
        out_specs=(vmem,) + (hbm,) * 5,
        scratch_shapes=[
            pltpu.VMEM((4, count), I32),
            pltpu.VMEM((8, count), I32),
            pltpu.VMEM((8, count), F32),
            pltpu.VMEM((count, width), BF16),
            pltpu.VMEM((width, inner), BF16),
            pltpu.VMEM((width, inner), BF16),
            pltpu.VMEM((inner, width), BF16),
            pltpu.VMEM((CHUNKS, HALF, count), BF16),
            pltpu.VMEM((CHUNKS, HALF, width + EXT), BF16),
            pltpu.VMEM((CHUNKS, 2 * HALF, width + EXT), BF16),
            pltpu.VMEM((2 * HALF, inner), BF16),
            pltpu.VMEM((CHUNKS, HALF, width), BF16),
            pltpu.VMEM((HALF, width), BF16),
            pltpu.VMEM((CHUNKS, HALF, width), BF16),
            pltpu.VMEM((count, width), F32),
            pltpu.VMEM((blocks, deep, lanes), F32),
            pltpu.VMEM((blocks, deep, lanes), F32),
            pltpu.VMEM((blocks, deep, lanes), BF16),
            pltpu.VMEM((CHIPS, deep, lanes), BF16),
            pltpu.VMEM((deep, lanes), F32),
            dma((4,)), dma((3,)),
            per_chunk, per_chunk, per_chunk, dma((2,)), per_chunk, per_chunk, per_chunk,
            per_chunk, per_chunk, per_chunk, per_chunk, per_chunk, per_chunk,
            dma, dma, dma, dma, dma, dma, dma, dma,
        ],
        compiler_params=pltpu.CompilerParams(
            collective_id=0, has_side_effects=True, vmem_limit_bytes=67043328
        ),
        cost_estimate=pl.CostEstimate(
            flops=12 * CHIPS * CAP * width * inner, bytes_accessed=50 << 20, transcendentals=0
        ),
    )(
        node_ids.T, local_ids.T, affinity.T, tokens, w_gate, w_up, w_down,
        grad_parts.reshape(2, blocks, deep, lanes),
    )
    return outs[0], outs[1]


def solution(mesh):
    spec2 = P(("edp", "ep"), None)
    spec3 = P(("edp", "ep"), None, None)
    return jax.shard_map(
        body,
        mesh=mesh,
        in_specs=(spec2,) * 4 + (spec3,) * 4,
        out_specs=(spec2, spec2),
        check_vma=False,
    )
```

time: 591 us -> 135 us (0.23)
  the two profiles are of different devices: /device:TPU:42 before, /device:TPU:0 now
where the time goes in v2:
time: 135 us
  Pallas kernels  131 us (97%)
  local copies, waits for them, and re-layouts  3.48 us (3%)
    pallas_call x1, Pallas kernels, body(): pl.pallas_call(moe_body, name='moe', out_shape=(jax.ShapeDtypeStruct((cou...  131 us
    unnamed x2, local copies, waits for them, and re-layouts  3.48 us

profile of v2, /device:TPU:0, one launch (start us, length us, event | category | flops | bytes accessed | tf_op | source)
XLA Modules:
  0.0 134.9 jit_solution(34234861272616213)
XLA Ops:
  0.6 130.8 %moe.1 = (bf16[128,3584]{1,0:T(8,128)(2,1)}, f32[28,128]{1,0:T(8,128)}, bf16[2,32,5,2,3712]{4,3,2,1,0:T(2,128)(2,1)}, bf16[2,32,5,2,3712]{4,3,2,1,0:T(2,128)(2,1...) custom-call(s32[4,128]{1,0:T(4,128)} %bitcast.7, s32[8,128]{1,0:T(8,128)} %bitcast.5, ...), custom_call_target="tpu_custom_call" | custom-call | flops 28185722880 | bytes 52428800 | tf_op jit(solution)/shard_map/moe/pallas_call | solution.py:406
  131.4 2.2 %copy.12 = bf16[128,3584]{1,0:T(8,128)(2,1)} copy(bf16[128,3584]{1,0:T(8,128)(2,1)} %get-tuple-element.8) | data formatting | bytes 1835008
  133.6 1.3 copy.13

commit v3 on v2

--- a/solution.py
+++ b/solution.py
@@ -7,6 +7,7 @@
 
 MESH = pl.DeviceIdType.MESH
 CHUNKS = 2
+HOLD = 0
 CHIPS = 64
 PER = CHIPS // CHUNKS
 CAP = 10
@@ -14,6 +15,8 @@
 PAIRS = CAP // 2
 EXT = 128
 TILE = 256
+WIDE = 512
+PARTS = ((0, 2048), (2048, 1536))
 BF16 = jnp.bfloat16
 F32 = jnp.float32
 I32 = jnp.int32
@@ -64,11 +67,11 @@
 
 def moe_body(
     nodes, locals_, aff, tokens, w_gate, w_up, w_down, grads,
-    mixed, router, send, land, pair_out, back,
+    mixed, router, size_in, size_out,
     node_v, local_v, aff_v, tok_v, gate_v, up_v, down_v, hot, rows, xs, hidden, theirs, mine,
-    other, acc, g_mine, g_other, g_sum, g_in, g_tot,
-    in_sems, w_sems, row_sems, disp_send, disp_recv, own_sems, fwd_send, fwd_recv, x_sems,
-    out_send, out_recv, p_sems, back_send, back_recv, mix_sems,
+    other, back, acc, g_mine, g_other, g_sum, g_in, g_tot,
+    in_sems, w_sems, disp_send, disp_recv, fwd_send, fwd_recv,
+    out_send, out_recv, back_send, back_recv,
     g_load, g_swap_send, g_swap_recv, g_send, g_recv, g_out, g_out_send, g_out_recv,
 ):
     x, y, z, core = place()
@@ -95,15 +98,6 @@
 
     lax.fori_loop(1, CHIPS, greet, 0)
     pl.semaphore_signal(barrier, 1, device_id=partner, device_id_type=MESH)
-    g_take = pltpu.make_async_copy(grads.at[core], g_mine, g_load)
-    g_take.start()
-    loads = [
-        pltpu.make_async_copy(w_gate.at[0], gate_v, w_sems.at[0]),
-        pltpu.make_async_copy(w_up.at[0], up_v, w_sems.at[1]),
-        pltpu.make_async_copy(w_down.at[0], down_v, w_sems.at[2]),
-    ]
-    for load in loads:
-        load.start()
     for load in small:
         load.wait()
 
@@ -161,18 +155,16 @@
             rows[chunk, :, k * part : (k + 1) * part] = jnp.dot(
                 one_hot, tok_v[:, k * part : (k + 1) * part], preferred_element_type=F32
             ).astype(BF16)
-        copy = pltpu.make_async_copy(
-            rows.at[chunk], send.at[chunk].reshape(HALF, width + EXT), row_sems.at[chunk]
-        )
-        copy.start()
-        return copy
+
+    def two(ref, chunk, q, p):
+        return ref.at[chunk, pl.ds(pl.multiple_of(q * CAP + p * 2, 2), 2)]
 
     def dispatch(chunk):
         def step(p, carry):
             for o in ORDER[chunk]:
                 q = slot_of(*o)[1]
                 pltpu.make_async_remote_copy(
-                    send.at[chunk, q, p], land.at[chunk, q, p],
+                    two(rows, chunk, q, p), two(xs, chunk, q, p),
                     disp_send.at[chunk], disp_recv.at[chunk],
                     device_id=device(x + o[0], y + o[1], z + o[2], core), device_id_type=MESH,
                 ).start()
@@ -180,20 +172,27 @@
 
         lax.fori_loop(0, PAIRS, step, 0)
 
-    filled = fill(0)
+    fill(0)
     pl.semaphore_wait(barrier, CHIPS)
+    dispatch(0)
+    g_take = pltpu.make_async_copy(grads.at[core], g_mine, g_load)
+    g_take.start()
     g_swap = pltpu.make_async_remote_copy(
         grads.at[1 - core], g_other, g_swap_send, g_swap_recv,
         device_id=partner, device_id_type=MESH,
     )
     g_swap.start()
-    filled.wait()
-    own = pltpu.make_async_copy(send.at[0, 0], land.at[0, 0], own_sems.at[0])
-    own.start()
-    dispatch(0)
+    loads = [
+        pltpu.make_async_copy(w_gate.at[0], gate_v, w_sems.at[0]),
+        pltpu.make_async_copy(w_up.at[0], up_v, w_sems.at[1]),
+        pltpu.make_async_copy(w_down.at[0], down_v, w_sems.at[2]),
+    ]
+    for load in loads:
+        load.start()
     for chunk in range(1, CHUNKS):
-        fill(chunk).wait()
+        fill(chunk)
         dispatch(chunk)
+    xs[0, :CAP, :] = rows[0, :CAP, :]
 
     blocks = g_sum.shape[0]
     home_chip = z * 16 + x * 4 + y
@@ -226,63 +225,60 @@
 
     lax.fori_loop(0, blocks, g_push, 0)
 
+    def dispatched(chunk):
+        first = 1 if chunk == 0 else 0
+        many(size_in.at[pl.ds(first, PER - first)], disp_send.at[chunk]).wait()
+
+    def go_home(chunk):
+        def home(p, carry):
+            for o in ORDER[chunk]:
+                q = slot_of(*o)[1]
+                pltpu.make_async_remote_copy(
+                    two(rows.at[:, :, pl.ds(0, width)], chunk, q, p), two(back, chunk, q, p),
+                    back_send.at[chunk], back_recv.at[chunk],
+                    device_id=device(x + 4 - o[0], y + 4 - o[1], z + 4 - o[2], core),
+                    device_id_type=MESH,
+                ).start()
+            return carry
+
+        lax.fori_loop(0, PAIRS, home, 0)
+
     forwards, swaps = [], []
-    keep = None
     for chunk in range(CHUNKS):
         first = 1 if chunk == 0 else 0
-        if chunk == 0:
-            own.wait()
-        many(land.at[chunk, pl.ds(first, PER - first)], disp_recv.at[chunk]).wait()
-        rows_in = land.at[chunk].reshape(HALF, width + EXT)
+        many(size_in.at[pl.ds(first, PER - first)], disp_recv.at[chunk]).wait()
         forward = pltpu.make_async_remote_copy(
-            rows_in, xs.at[chunk, pl.ds(HALF, HALF)], fwd_send.at[chunk], fwd_recv.at[chunk],
-            device_id=partner, device_id_type=MESH,
+            xs.at[chunk, pl.ds(0, HALF)], xs.at[chunk, pl.ds(HALF, HALF)],
+            fwd_send.at[chunk], fwd_recv.at[chunk], device_id=partner, device_id_type=MESH,
         )
         forward.start()
         forwards.append(forward)
-        take = pltpu.make_async_copy(rows_in, xs.at[chunk, pl.ds(0, HALF)], x_sems.at[chunk])
-        take.start()
         if chunk == 0:
             loads[0].wait()
             loads[1].wait()
-        take.wait()
         forward.wait_recv()
 
-        def gate_step(n, carry):
-            cols = tile_at(n)
+        for n in range(gate_v.shape[1] // WIDE):
+            cols = slice(n * WIDE, (n + 1) * WIDE)
             block = xs[chunk, :, :width]
             gate = jnp.dot(block, gate_v[:, cols], preferred_element_type=F32)
             up = jnp.dot(block, up_v[:, cols], preferred_element_type=F32)
             hidden[:, cols] = (gate / (1.0 + jnp.exp(-gate)) * up).astype(BF16)
-            return carry
-
-        lax.fori_loop(0, gate_v.shape[1] // TILE, gate_step, 0)
         if chunk == 0:
             loads[2].wait()
 
-        def their_step(n, carry):
-            cols = tile_at(n)
-            theirs[chunk, :, cols] = jnp.dot(
-                hidden[HALF:, :], down_v[:, cols], preferred_element_type=F32
-            ).astype(BF16)
-            return carry
-
-        lax.fori_loop(0, width // TILE, their_step, 0)
-        swap = pltpu.make_async_remote_copy(
-            theirs.at[chunk], other.at[chunk], out_send.at[chunk], out_recv.at[chunk],
-            device_id=partner, device_id_type=MESH,
-        )
-        swap.start()
-        swaps.append(swap)
-
-        def mine_step(n, carry):
-            cols = tile_at(n)
-            mine[:, cols] = jnp.dot(
-                hidden[:HALF, :], down_v[:, cols], preferred_element_type=F32
-            ).astype(BF16)
-            return carry
-
-        lax.fori_loop(0, width // TILE, mine_step, 0)
+        for n, (start, size) in enumerate(PARTS):
+            cols = slice(start, start + size)
+            both = jnp.dot(hidden[...], down_v[:, cols], preferred_element_type=F32).astype(BF16)
+            theirs[chunk, :, cols] = both[HALF:]
+            mine[:, cols] = both[:HALF]
+            swap = pltpu.make_async_remote_copy(
+                theirs.at[chunk, :, pl.ds(start, size)], other.at[chunk, :, pl.ds(start, size)],
+                out_send.at[chunk, n], out_recv.at[chunk, n],
+                device_id=partner, device_id_type=MESH,
+            )
+            swap.start()
+            swaps.append(swap)
         ext = xs[chunk, :HALF, width:].astype(F32)
         lane = lax.broadcasted_iota(I32, ext.shape, 1)
         even = jnp.sum(jnp.where(lane < 3, ext, 0.0), axis=1, keepdims=True)
@@ -290,7 +286,8 @@
         is_even = (lax.broadcasted_iota(I32, even.shape, 0) * 0 + core) == 0
         w_mine = jnp.where(is_even, even, odd)
         w_other = jnp.where(is_even, odd, even)
-        swap.wait_recv()
+        if chunk <= HOLD:
+            dispatched(chunk)
 
         def sum_step(n, carry):
             cols = tile_at(n)
@@ -299,29 +296,17 @@
             ).astype(BF16)
             return carry
 
-        lax.fori_loop(0, width // TILE, sum_step, 0)
-        put = pltpu.make_async_copy(
-            rows.at[chunk, :, pl.ds(0, width)], pair_out.at[chunk].reshape(HALF, width),
-            p_sems.at[chunk],
-        )
-        put.start()
-        put.wait()
-
-        def home(p, carry):
-            for o in ORDER[chunk]:
-                q = slot_of(*o)[1]
-                pltpu.make_async_remote_copy(
-                    pair_out.at[chunk, q, p], back.at[chunk, q, p],
-                    back_send.at[chunk], back_recv.at[chunk],
-                    device_id=device(x + 4 - o[0], y + 4 - o[1], z + 4 - o[2], core),
-                    device_id_type=MESH,
-                ).start()
-            return carry
-
-        lax.fori_loop(0, PAIRS, home, 0)
+        for n, (start, size) in enumerate(PARTS):
+            swaps[chunk * len(PARTS) + n].wait_recv()
+            lax.fori_loop(start // TILE, (start + size) // TILE, sum_step, 0)
         if chunk == 0:
-            keep = pltpu.make_async_copy(pair_out.at[0, 0], back.at[0, 0], own_sems.at[1])
-            keep.start()
+            back[0, :CAP, :] = rows[0, :CAP, :width]
+        if chunk == HOLD:
+            for later in range(chunk + 1, CHUNKS):
+                dispatched(later)
+        for ready in range(CHUNKS):
+            if ready == chunk > HOLD or ready <= chunk == HOLD:
+                go_home(ready)
 
     @pl.when(holder)
     def _():
@@ -347,21 +332,14 @@
 
         lax.fori_loop(0, 7, g_give, 0)
 
-    keep.wait()
     for chunk in range(CHUNKS):
         first = 1 if chunk == 0 else 0
-        many(back.at[chunk, pl.ds(first, PER - first)], back_recv.at[chunk]).wait()
-        fetch = pltpu.make_async_copy(
-            back.at[chunk].reshape(HALF, width), xs.at[chunk, pl.ds(0, HALF), pl.ds(0, width)],
-            mix_sems.at[chunk],
-        )
-        fetch.start()
-        fetch.wait()
+        many(size_out.at[pl.ds(first, PER - first)], back_recv.at[chunk]).wait()
         part = width // 4
         for k in range(4):
             cols = slice(k * part, (k + 1) * part)
             value = lax.dot_general(
-                hot[chunk], xs[chunk, :HALF, cols], TURN, preferred_element_type=F32
+                hot[chunk], back[chunk, :, cols], TURN, preferred_element_type=F32
             )
             if chunk:
                 value = acc[:, cols] + value
@@ -386,9 +364,14 @@
     for chunk in range(CHUNKS):
         first = 1 if chunk == 0 else 0
         forwards[chunk].wait_send()
-        swaps[chunk].wait_send()
-        many(send.at[chunk, pl.ds(first, PER - first)], disp_send.at[chunk]).wait()
-        many(pair_out.at[chunk, pl.ds(first, PER - first)], back_send.at[chunk]).wait()
+        for n in range(len(PARTS)):
+            swaps[chunk * len(PARTS) + n].wait_send()
+        many(size_out.at[pl.ds(first, PER - first)], back_send.at[chunk]).wait()
+
+
+def finish_body(mixed_in, router_in, mixed, router):
+    mixed[...] = mixed_in[...]
+    router[...] = router_in[...]
 
 
 def body(tokens, node_ids, local_ids, affinity, w_gate, w_up, w_down, grad_parts):
@@ -401,18 +384,18 @@
     blocks = CHIPS // 2
     deep = grad_parts.shape[1] // CHIPS
     lanes = grad_parts.shape[2]
-    wide = jax.ShapeDtypeStruct((CHUNKS, PER, PAIRS, 2, width + EXT), BF16)
-    plain = jax.ShapeDtypeStruct((CHUNKS, PER, PAIRS, 2, width), BF16)
+    wide = jax.ShapeDtypeStruct((PER, PAIRS, 2, width + EXT), BF16)
+    plain = jax.ShapeDtypeStruct((PER, PAIRS, 2, width), BF16)
     outs = pl.pallas_call(
         moe_body,
         name="moe",
         out_shape=(
             jax.ShapeDtypeStruct((count, width), BF16),
             jax.ShapeDtypeStruct((deep // 2, lanes), F32),
-            wide, wide, plain, plain,
+            wide, plain,
         ),
         in_specs=[hbm] * 8,
-        out_specs=(vmem,) + (hbm,) * 5,
+        out_specs=(vmem,) + (hbm,) * 3,
         scratch_shapes=[
             pltpu.VMEM((4, count), I32),
             pltpu.VMEM((8, count), I32),
@@ -428,6 +411,7 @@
             pltpu.VMEM((CHUNKS, HALF, width), BF16),
             pltpu.VMEM((HALF, width), BF16),
             pltpu.VMEM((CHUNKS, HALF, width), BF16),
+            pltpu.VMEM((CHUNKS, HALF, width), BF16),
             pltpu.VMEM((count, width), F32),
             pltpu.VMEM((blocks, deep, lanes), F32),
             pltpu.VMEM((blocks, deep, lanes), F32),
@@ -435,8 +419,8 @@
             pltpu.VMEM((CHIPS, deep, lanes), BF16),
             pltpu.VMEM((deep, lanes), F32),
             dma((4,)), dma((3,)),
-            per_chunk, per_chunk, per_chunk, dma((2,)), per_chunk, per_chunk, per_chunk,
-            per_chunk, per_chunk, per_chunk, per_chunk, per_chunk, per_chunk,
+            per_chunk, per_chunk, per_chunk, per_chunk,
+            dma((CHUNKS, len(PARTS))), dma((CHUNKS, len(PARTS))), per_chunk, per_chunk,
             dma, dma, dma, dma, dma, dma, dma, dma,
         ],
         compiler_params=pltpu.CompilerParams(
@@ -449,7 +433,16 @@
         node_ids.T, local_ids.T, affinity.T, tokens, w_gate, w_up, w_down,
         grad_parts.reshape(2, blocks, deep, lanes),
     )
-    return outs[0], outs[1]
+    return pl.pallas_call(
+        finish_body,
+        name="finish",
+        out_shape=(
+            jax.ShapeDtypeStruct((count, width), BF16),
+            jax.ShapeDtypeStruct((deep // 2, lanes), F32),
+        ),
+        in_specs=[vmem, vmem],
+        out_specs=(vmem, vmem),
+    )(outs[0], outs[1])
 
 
 def solution(mesh):

time: 135 us -> 124 us (0.919)
  Pallas kernels: 131 us -> 123 us
  local copies, waits for them, and re-layouts: 3.48 us -> 0 us
    pallas_call x1, Pallas kernels: 131 us -> 121 us  [body(): pl.pallas_call(moe_body, name='moe', out_shape=(jax.ShapeDtypeStruct((cou...]
    unnamed x2 -> x0, local copies, waits for them, and re-layouts: 3.48 us -> none
    pallas_call x0 -> x1, Pallas kernels: none -> 2.17 us  [body(): pl.pallas_call(finish_body, name='finish', out_shape=(jax.ShapeDtypeStruc...]
where the time goes in v3:
time: 124 us; the launch traced here: 123 us
  Pallas kernels  123 us (99%)
    pallas_call x1, Pallas kernels, body(): pl.pallas_call(moe_body, name='moe', out_shape=(jax.ShapeDtypeStruct((cou...  121 us

profile of v3, /device:TPU:0, one launch (start us, length us, event | category | flops | bytes accessed | tf_op | source)
XLA Modules:
  0.0 123.4 jit_solution(8271648419230985426)
XLA Ops:
  0.6 120.6 %moe.1 = (bf16[128,3584]{1,0:T(8,128)(2,1)}, f32[28,128]{1,0:T(8,128)}, bf16[32,5,2,3712]{3,2,1,0:T(2,128)(2,1)}, bf16[32,5,2,3584]{3,2,1,0:T(2,128)(2,1)}) custom-call(s32[4,128]{1,0:T(4,128)} %bitcast.7, s32[8,128]{1,0:T(8,128)} %bitcast.5, f32[8,128]{1,0:T(8,128)} %bitcast.6, bf16[128,3584]{1,0:T(8,128)(2,1)} %tokens.1, bf16[1,3584,1024]{2,1,0:T(8,128)(2,1)} %w_gate.1, ...), custom_call_target="tpu_custom_call" | custom-call | flops 28185722880 | bytes 52428800 | tf_op jit(solution)/shard_map/moe/pallas_call | solution.py:389
  121.3 2.2 %finish.1 = (bf16[128,3584]{1,0:T(8,128)(2,1)}, f32[28,128]{1,0:T(8,128)}) custom-call(bf16[128,3584]{1,0:T(8,128)(2,1)} %get-tuple-element.4.mixed_in, f32[28,128]{1,0:T(8,128)} %get-tuple-element.5.router_in), custom_call_target="tpu_custom_call" | custom-call | tf_op jit(solution)/shard_map/finish/pallas_call | solution.py:436

commit v4 on v3

--- a/solution.py
+++ b/solution.py
@@ -13,7 +13,7 @@
 CAP = 10
 HALF = PER * CAP
 PAIRS = CAP // 2
-EXT = 128
+PARTIES = 4 // CHUNKS
 TILE = 256
 WIDE = 512
 PARTS = ((0, 2048), (2048, 1536))
@@ -36,7 +36,8 @@
 
 
 def slot_of(dx, dy, dz):
-    return (dx + dy + dz) % CHUNKS, (dx * 4 + dy) * (4 // CHUNKS) + dz // CHUNKS
+    kind = (dx + dy + dz) % 4
+    return kind % CHUNKS, kind // CHUNKS * 16 + dx * 4 + dy
 
 
 def send_order():
@@ -67,11 +68,11 @@
 
 def moe_body(
     nodes, locals_, aff, tokens, w_gate, w_up, w_down, grads,
-    mixed, router, size_in, size_out,
+    mixed, router, size_in,
     node_v, local_v, aff_v, tok_v, gate_v, up_v, down_v, hot, rows, xs, hidden, theirs, mine,
-    other, back, acc, g_mine, g_other, g_sum, g_in, g_tot,
+    other, back, acc, w_out, w_in, g_mine, g_other, g_sum, g_in, g_tot,
     in_sems, w_sems, disp_send, disp_recv, fwd_send, fwd_recv,
-    out_send, out_recv, back_send, back_recv,
+    out_send, out_recv, back_send, back_recv, wt_send, wt_recv,
     g_load, g_swap_send, g_swap_recv, g_send, g_recv, g_out, g_out_send, g_out_recv,
 ):
     x, y, z, core = place()
@@ -113,48 +114,61 @@
         dx = (((pair >> 2) & 3) - x + 4) & 3
         dy = ((pair & 3) - y + 4) & 3
         dz = (pz - z + 4) & 3
-        chunk = (dx + dy + dz) & (CHUNKS - 1)
-        off = chunk * PER + (dx * 4 + dy) * (4 // CHUNKS) + dz // CHUNKS
+        kind = (dx + dy + dz) & 3
+        off = (kind & (CHUNKS - 1)) * PER + (kind // CHUNKS) * 16 + dx * 4 + dy
         offsets.append(off)
         hit = hit + (chip_id == off).astype(F32)
     row = lax.broadcasted_iota(I32, (count, count), 0)
     col = lax.broadcasted_iota(I32, (count, count), 1)
     earlier = (row < col).astype(F32).astype(BF16)
     before = jnp.dot(hit.astype(BF16), earlier, preferred_element_type=F32)
-    slots, pieces = [], []
-    for j in range(4):
-        rank = jnp.sum(jnp.where(chip_id == offsets[j], before, 0.0), axis=0, keepdims=True)
-        slots.append(offsets[j] * CAP + rank.astype(I32))
-        lead_even = (local[2 * j : 2 * j + 1, :] & 1) == 0
-        first, second = weight[2 * j : 2 * j + 1, :], weight[2 * j + 1 : 2 * j + 2, :]
-        parts = jnp.zeros((EXT, count), F32)
-        for k, value in enumerate(
-            (jnp.where(lead_even, first, second), jnp.where(lead_even, second, first))
-        ):
-            for part in range(3):
-                piece = value.astype(BF16).astype(F32)
-                parts = jnp.where(row == 3 * k + part, piece, parts)
-                value = value - piece
-        pieces.append(parts.astype(BF16))
+    ranks = [
+        jnp.sum(jnp.where(chip_id == offsets[j], before, 0.0), axis=0, keepdims=True).astype(I32)
+        for j in range(4)
+    ]
 
     def fill(chunk):
         slot_id = lax.broadcasted_iota(I32, (HALF, count), 0) + chunk * HALF
         total = jnp.zeros((HALF, count), F32)
-        ext = jnp.zeros((HALF, EXT), F32)
         for j in range(4):
-            match = (slot_id == slots[j]).astype(F32)
-            total = total + match
-            ext = ext + lax.dot_general(
-                match.astype(BF16), pieces[j], SIDE, preferred_element_type=F32
-            )
+            total = total + (slot_id == offsets[j] * CAP + ranks[j]).astype(F32)
         one_hot = total.astype(BF16)
         hot[chunk] = one_hot
-        rows[chunk, :, width:] = ext.astype(BF16)
         part = width // 4
         for k in range(4):
             rows[chunk, :, k * part : (k + 1) * part] = jnp.dot(
                 one_hot, tok_v[:, k * part : (k + 1) * part], preferred_element_type=F32
             ).astype(BF16)
+
+    def spread_weights():
+        total = jnp.zeros((CHIPS, count), F32)
+        for j in range(4):
+            lead_even = (local[2 * j : 2 * j + 1, :] & 1) == 0
+            first, second = weight[2 * j : 2 * j + 1, :], weight[2 * j + 1 : 2 * j + 2, :]
+            match = chip_id == offsets[j]
+            for shift, value in (
+                (0, jnp.where(lead_even, first, second)),
+                (16, jnp.where(lead_even, second, first)),
+            ):
+                lanes = (row == ranks[j] + shift).astype(F32).astype(BF16)
+                for part in range(3):
+                    piece = value.astype(BF16).astype(F32)
+                    value = value - piece
+                    total = total + lax.dot_general(
+                        jnp.where(match, piece, 0.0).astype(BF16), lanes, SIDE,
+                        preferred_element_type=F32,
+                    )
+        w_out[...] = total.reshape(CHIPS, 1, count)
+
+    def push_weights():
+        for chunk in range(CHUNKS):
+            for o in ORDER[chunk]:
+                n = chunk * PER + slot_of(*o)[1]
+                pltpu.make_async_remote_copy(
+                    w_out.at[n], w_in.at[n], wt_send, wt_recv,
+                    device_id=device(x + o[0], y + o[1], z + o[2], core), device_id_type=MESH,
+                ).start()
+        w_in[0] = w_out[0]
 
     def two(ref, chunk, q, p):
         return ref.at[chunk, pl.ds(pl.multiple_of(q * CAP + p * 2, 2), 2)]
@@ -192,7 +206,9 @@
     for chunk in range(1, CHUNKS):
         fill(chunk)
         dispatch(chunk)
-    xs[0, :CAP, :] = rows[0, :CAP, :]
+    xs[0, :CAP] = rows[0, :CAP]
+    spread_weights()
+    push_weights()
 
     blocks = g_sum.shape[0]
     home_chip = z * 16 + x * 4 + y
@@ -234,8 +250,8 @@
             for o in ORDER[chunk]:
                 q = slot_of(*o)[1]
                 pltpu.make_async_remote_copy(
-                    two(rows.at[:, :, pl.ds(0, width)], chunk, q, p), two(back, chunk, q, p),
-                    back_send.at[chunk], back_recv.at[chunk],
+                    two(rows, chunk, q, p), two(back, chunk, q, p),
+                    back_send.at[chunk, q // 16], back_recv.at[chunk, q // 16],
                     device_id=device(x + 4 - o[0], y + 4 - o[1], z + 4 - o[2], core),
                     device_id_type=MESH,
                 ).start()
@@ -260,7 +276,7 @@
 
         for n in range(gate_v.shape[1] // WIDE):
             cols = slice(n * WIDE, (n + 1) * WIDE)
-            block = xs[chunk, :, :width]
+            block = xs[chunk]
             gate = jnp.dot(block, gate_v[:, cols], preferred_element_type=F32)
             up = jnp.dot(block, up_v[:, cols], preferred_element_type=F32)
             hidden[:, cols] = (gate / (1.0 + jnp.exp(-gate)) * up).astype(BF16)
@@ -279,10 +295,21 @@
             )
             swap.start()
             swaps.append(swap)
-        ext = xs[chunk, :HALF, width:].astype(F32)
-        lane = lax.broadcasted_iota(I32, ext.shape, 1)
-        even = jnp.sum(jnp.where(lane < 3, ext, 0.0), axis=1, keepdims=True)
-        odd = jnp.sum(jnp.where(lane < 3, 0.0, ext), axis=1, keepdims=True)
+        if chunk == 0:
+            many(w_in.at[pl.ds(0, CHIPS - 1)], wt_recv).wait()
+        spread = w_in[chunk * PER : (chunk + 1) * PER].reshape(PER, count)
+        at = lax.broadcasted_iota(I32, (HALF, PER), 0)
+        source = (((at * 205) >> 11) == lax.broadcasted_iota(I32, (HALF, PER), 1)).astype(F32)
+        table = jnp.zeros((HALF, count), F32)
+        for _ in range(3):
+            piece = spread.astype(BF16)
+            spread = spread - piece.astype(F32)
+            table = table + jnp.dot(source.astype(BF16), piece, preferred_element_type=F32)
+        at = lax.broadcasted_iota(I32, (HALF, count), 0)
+        lane = lax.broadcasted_iota(I32, (HALF, count), 1)
+        inside = at - ((at * 205) >> 11) * CAP
+        even = jnp.sum(jnp.where(lane == inside, table, 0.0), axis=1, keepdims=True)
+        odd = jnp.sum(jnp.where(lane == inside + 16, table, 0.0), axis=1, keepdims=True)
         is_even = (lax.broadcasted_iota(I32, even.shape, 0) * 0 + core) == 0
         w_mine = jnp.where(is_even, even, odd)
         w_other = jnp.where(is_even, odd, even)
@@ -300,7 +327,7 @@
             swaps[chunk * len(PARTS) + n].wait_recv()
             lax.fori_loop(start // TILE, (start + size) // TILE, sum_step, 0)
         if chunk == 0:
-            back[0, :CAP, :] = rows[0, :CAP, :width]
+            back[0, :CAP] = rows[0, :CAP]
         if chunk == HOLD:
             for later in range(chunk + 1, CHUNKS):
                 dispatched(later)
@@ -332,18 +359,20 @@
 
         lax.fori_loop(0, 7, g_give, 0)
 
-    for chunk in range(CHUNKS):
-        first = 1 if chunk == 0 else 0
-        many(size_out.at[pl.ds(first, PER - first)], back_recv.at[chunk]).wait()
+    for step in range(CHUNKS * PARTIES):
+        chunk, party = step // PARTIES, step % PARTIES
+        first = 1 if step == 0 else 0
+        many(size_in.at[pl.ds(first, 16 - first)], back_recv.at[chunk, party]).wait()
+        lot = slice(party * 16 * CAP, (party + 1) * 16 * CAP)
         part = width // 4
         for k in range(4):
             cols = slice(k * part, (k + 1) * part)
             value = lax.dot_general(
-                hot[chunk], back[chunk, :, cols], TURN, preferred_element_type=F32
+                hot[chunk, lot], back[chunk, lot, cols], TURN, preferred_element_type=F32
             )
-            if chunk:
+            if step:
                 value = acc[:, cols] + value
-            if chunk == CHUNKS - 1:
+            if step == CHUNKS * PARTIES - 1:
                 mixed[:, cols] = value.astype(BF16)
             else:
                 acc[:, cols] = value
@@ -361,17 +390,15 @@
         many(g_sum.at[0], g_send).wait()
         many(g_sum.at[0], g_out_recv).wait()
 
+    many(w_out.at[pl.ds(0, CHIPS - 1)], wt_send).wait()
     for chunk in range(CHUNKS):
         first = 1 if chunk == 0 else 0
         forwards[chunk].wait_send()
         for n in range(len(PARTS)):
             swaps[chunk * len(PARTS) + n].wait_send()
-        many(size_out.at[pl.ds(first, PER - first)], back_send.at[chunk]).wait()
-
-
-def finish_body(mixed_in, router_in, mixed, router):
-    mixed[...] = mixed_in[...]
-    router[...] = router_in[...]
+        for party in range(PARTIES):
+            skip = first if party == 0 else 0
+            many(size_in.at[pl.ds(skip, 16 - skip)], back_send.at[chunk, party]).wait()
 
 
 def body(tokens, node_ids, local_ids, affinity, w_gate, w_up, w_down, grad_parts):
@@ -384,18 +411,17 @@
     blocks = CHIPS // 2
     deep = grad_parts.shape[1] // CHIPS
     lanes = grad_parts.shape[2]
-    wide = jax.ShapeDtypeStruct((PER, PAIRS, 2, width + EXT), BF16)
     plain = jax.ShapeDtypeStruct((PER, PAIRS, 2, width), BF16)
     outs = pl.pallas_call(
         moe_body,
         name="moe",
         out_shape=(
-            jax.ShapeDtypeStruct((count, width), BF16),
-            jax.ShapeDtypeStruct((deep // 2, lanes), F32),
-            wide, plain,
+            pltpu.VMEM((count, width), BF16),
+            pltpu.VMEM((deep // 2, lanes), F32),
+            plain,
         ),
         in_specs=[hbm] * 8,
-        out_specs=(vmem,) + (hbm,) * 3,
+        out_specs=(vmem, vmem, hbm),
         scratch_shapes=[
             pltpu.VMEM((4, count), I32),
             pltpu.VMEM((8, count), I32),
@@ -405,14 +431,16 @@
             pltpu.VMEM((width, inner), BF16),
             pltpu.VMEM((inner, width), BF16),
             pltpu.VMEM((CHUNKS, HALF, count), BF16),
-            pltpu.VMEM((CHUNKS, HALF, width + EXT), BF16),
-            pltpu.VMEM((CHUNKS, 2 * HALF, width + EXT), BF16),
+            pltpu.VMEM((CHUNKS, HALF, width), BF16),
+            pltpu.VMEM((CHUNKS, 2 * HALF, width), BF16),
             pltpu.VMEM((2 * HALF, inner), BF16),
             pltpu.VMEM((CHUNKS, HALF, width), BF16),
             pltpu.VMEM((HALF, width), BF16),
             pltpu.VMEM((CHUNKS, HALF, width), BF16),
             pltpu.VMEM((CHUNKS, HALF, width), BF16),
             pltpu.VMEM((count, width), F32),
+            pltpu.VMEM((CHIPS, 1, count), F32),
+            pltpu.VMEM((CHIPS, 1, count), F32),
             pltpu.VMEM((blocks, deep, lanes), F32),
             pltpu.VMEM((blocks, deep, lanes), F32),
             pltpu.VMEM((blocks, deep, lanes), BF16),
@@ -420,11 +448,12 @@
             pltpu.VMEM((deep, lanes), F32),
             dma((4,)), dma((3,)),
             per_chunk, per_chunk, per_chunk, per_chunk,
-            dma((CHUNKS, len(PARTS))), dma((CHUNKS, len(PARTS))), per_chunk, per_chunk,
+            dma((CHUNKS, len(PARTS))), dma((CHUNKS, len(PARTS))),
+            dma((CHUNKS, PARTIES)), dma((CHUNKS, PARTIES)), dma, dma,
             dma, dma, dma, dma, dma, dma, dma, dma,
         ],
         compiler_params=pltpu.CompilerParams(
-            collective_id=0, has_side_effects=True, vmem_limit_bytes=67043328
+            collective_id=0, has_side_effects=True, vmem_limit_bytes=64000000
         ),
         cost_estimate=pl.CostEstimate(
             flops=12 * CHIPS * CAP * width * inner, bytes_accessed=50 << 20, transcendentals=0
@@ -433,16 +462,7 @@
         node_ids.T, local_ids.T, affinity.T, tokens, w_gate, w_up, w_down,
         grad_parts.reshape(2, blocks, deep, lanes),
     )
-    return pl.pallas_call(
-        finish_body,
-        name="finish",
-        out_shape=(
-            jax.ShapeDtypeStruct((count, width), BF16),
-            jax.ShapeDtypeStruct((deep // 2, lanes), F32),
-        ),
-        in_specs=[vmem, vmem],
-        out_specs=(vmem, vmem),
-    )(outs[0], outs[1])
+    return outs[0], outs[1]
 
 
 def solution(mesh):

time: 124 us -> 122 us (0.984)
  Pallas kernels: 123 us -> 120 us
  local copies, waits for them, and re-layouts: 0 us -> 1.53 us
    pallas_call x2 -> x1, Pallas kernels: 123 us -> 120 us  [body(): pl.pallas_call(moe_body, name='moe', out_shape=(pltpu.VMEM((count, width)...]
    unnamed x0 -> x2, local copies, waits for them, and re-layouts: none -> 1.53 us
where the time goes in v4:
time: 122 us
  Pallas kernels  120 us (98%)
  local copies, waits for them, and re-layouts  1.53 us (1%)
    pallas_call x1, Pallas kernels, body(): pl.pallas_call(moe_body, name='moe', out_shape=(pltpu.VMEM((count, width)...  120 us

profile of v4, /device:TPU:0, one launch (start us, length us, event | category | flops | bytes accessed | tf_op | source)
XLA Modules:
  0.0 122.1 jit_solution(15739525873489938400)
XLA Ops:
  0.6 119.9 %moe.1 = (bf16[128,3584]{1,0:T(8,128)(2,1)S(1)}, f32[28,128]{1,0:T(8,128)S(1)}, bf16[32,5,2,3584]{3,2,1,0:T(2,128)(2,1)}) custom-call(s32[4,128]{1,0:T(4,128)} %bitcast.7, s32[8,128]{1,0:T(8,128)} %bitcast.5, f32[8,128]{1,0:T(8,128)} %bitcast.6, bf16[128,3584]{1,0:T(8,128)(2,1)} %tokens.1, bf16[1,3584,1024]{2,1,0:T(8,128)(2,1)} %w_gate.1, ...), custom_call_target="tpu_custom_call" | custom-call | flops 28185722880 | bytes 52428800 | tf_op jit(solution)/shard_map/moe/pallas_call | solution.py:415
  120.6 0.9 copy.12
  121.5 0.6 copy.13

commit v5 on v4

--- a/solution.py
+++ b/solution.py
@@ -91,13 +91,17 @@
         load.start()
     barrier = pltpu.get_barrier_semaphore()
 
-    def greet(n, carry):
-        pl.semaphore_signal(
-            barrier, 1, device_id=device(x + n // 16, y + n // 4, z + n, core), device_id_type=MESH
-        )
-        return carry
-
-    lax.fori_loop(1, CHIPS, greet, 0)
+    along_x = [(x + d) % 4 * 8 for d in range(4)]
+    along_y = [(y + d) % 4 * 2 + core for d in range(4)]
+    along_z = [(z + d) % 4 // 2 * 32 for d in range(4)]
+    halves = [(z + d) % 2 for d in range(2)]
+
+    def peer(o, sign=1):
+        dx, dy, dz = (sign * d % 4 for d in o)
+        return {"edp": halves[dz % 2], "ep": along_z[dz] + along_x[dx] + along_y[dy]}
+
+    for o in sorted(ORDER[0] + ORDER[1], key=lambda o: -sum(min(d, 4 - d) for d in o)):
+        pl.semaphore_signal(barrier, 1, device_id=peer(o), device_id_type=MESH)
     pl.semaphore_signal(barrier, 1, device_id=partner, device_id_type=MESH)
     for load in small:
         load.wait()
@@ -166,7 +170,7 @@
                 n = chunk * PER + slot_of(*o)[1]
                 pltpu.make_async_remote_copy(
                     w_out.at[n], w_in.at[n], wt_send, wt_recv,
-                    device_id=device(x + o[0], y + o[1], z + o[2], core), device_id_type=MESH,
+                    device_id=peer(o), device_id_type=MESH,
                 ).start()
         w_in[0] = w_out[0]
 
@@ -180,7 +184,7 @@
                 pltpu.make_async_remote_copy(
                     two(rows, chunk, q, p), two(xs, chunk, q, p),
                     disp_send.at[chunk], disp_recv.at[chunk],
-                    device_id=device(x + o[0], y + o[1], z + o[2], core), device_id_type=MESH,
+                    device_id=peer(o), device_id_type=MESH,
                 ).start()
             return carry
 
@@ -252,7 +256,7 @@
                 pltpu.make_async_remote_copy(
                     two(rows, chunk, q, p), two(back, chunk, q, p),
                     back_send.at[chunk, q // 16], back_recv.at[chunk, q // 16],
-                    device_id=device(x + 4 - o[0], y + 4 - o[1], z + 4 - o[2], core),
+                    device_id=peer(o, -1),
                     device_id_type=MESH,
                 ).start()
             return carry
@@ -260,7 +264,8 @@
         lax.fori_loop(0, PAIRS, home, 0)
 
     forwards, swaps = [], []
-    for chunk in range(CHUNKS):
+
+    def pass_on(chunk):
         first = 1 if chunk == 0 else 0
         many(size_in.at[pl.ds(first, PER - first)], disp_recv.at[chunk]).wait()
         forward = pltpu.make_async_remote_copy(
@@ -269,6 +274,11 @@
         )
         forward.start()
         forwards.append(forward)
+
+    for chunk in range(CHUNKS):
+        if chunk == 0:
+            pass_on(0)
+        forward = forwards[chunk]
         if chunk == 0:
             loads[0].wait()
             loads[1].wait()
@@ -331,6 +341,8 @@
         if chunk == HOLD:
             for later in range(chunk + 1, CHUNKS):
                 dispatched(later)
+        if chunk + 1 < CHUNKS:
+            pass_on(chunk + 1)
         for ready in range(CHUNKS):
             if ready == chunk > HOLD or ready <= chunk == HOLD:
                 go_home(ready)

time: 122 us -> 121 us (level)
  Pallas kernels: 120 us -> 118 us
    pallas_call x1, Pallas kernels: 120 us -> 118 us  [body(): pl.pallas_call(moe_body, name='moe', out_shape=(pltpu.VMEM((count, width)...]
where the time goes in v5:
time: 121 us
  Pallas kernels  118 us (98%)
  local copies, waits for them, and re-layouts  1.53 us (1%)
    pallas_call x1, Pallas kernels, body(): pl.pallas_call(moe_body, name='moe', out_shape=(pltpu.VMEM((count, width)...  118 us

profile of v5, /device:TPU:0, one launch (start us, length us, event | category | flops | bytes accessed | tf_op | source)
XLA Modules:
  0.0 120.5 jit_solution(14482320195730577461)
XLA Ops:
  0.6 118.4 %moe.1 = (bf16[128,3584]{1,0:T(8,128)(2,1)S(1)}, f32[28,128]{1,0:T(8,128)S(1)}, bf16[32,5,2,3584]{3,2,1,0:T(2,128)(2,1)}) custom-call(s32[4,128]{1,0:T(4,128)} %bitcast.7, s32[8,128]{1,0:T(8,128)} %bitcast.5, f32[8,128]{1,0:T(8,128)} %bitcast.6, bf16[128,3584]{1,0:T(8,128)(2,1)} %tokens.1, bf16[1,3584,1024]{2,1,0:T(8,128)(2,1)} %w_gate.1, ...), custom_call_target="tpu_custom_call" | custom-call | flops 28185722880 | bytes 52428800 | tf_op jit(solution)/shard_map/moe/pallas_call | solution.py:427
  119.0 0.9 copy.12
  119.9 0.6 copy.13

commit v6 on v5

--- a/solution.py
+++ b/solution.py
@@ -103,7 +103,7 @@
     for o in sorted(ORDER[0] + ORDER[1], key=lambda o: -sum(min(d, 4 - d) for d in o)):
         pl.semaphore_signal(barrier, 1, device_id=peer(o), device_id_type=MESH)
     pl.semaphore_signal(barrier, 1, device_id=partner, device_id_type=MESH)
-    for load in small:
+    for load in small[:3]:
         load.wait()
 
     affinity = aff_v[...]
@@ -190,6 +190,7 @@
 
         lax.fori_loop(0, PAIRS, step, 0)
 
+    small[3].wait()
     fill(0)
     pl.semaphore_wait(barrier, CHIPS)
     dispatch(0)

time: 121 us -> 121 us (level)
  no operation moved by 1% of the time
where the time goes in v6:
time: 121 us
  Pallas kernels  118 us (98%)
  local copies, waits for them, and re-layouts  1.53 us (1%)
    pallas_call x1, Pallas kernels, body(): pl.pallas_call(moe_body, name='moe', out_shape=(pltpu.VMEM((count, width)...  118 us

profile of v6, /device:TPU:0, one launch (start us, length us, event | category | flops | bytes accessed | tf_op | source)
XLA Modules:
  0.0 120.5 jit_solution(3832556795353650819)
XLA Ops:
  0.6 118.4 %moe.1 = (bf16[128,3584]{1,0:T(8,128)(2,1)S(1)}, f32[28,128]{1,0:T(8,128)S(1)}, bf16[32,5,2,3584]{3,2,1,0:T(2,128)(2,1)}) custom-call(s32[4,128]{1,0:T(4,128)} %bitcast.7, s32[8,128]{1,0:T(8,128)} %bitcast.5, f32[8,128]{1,0:T(8,128)} %bitcast.6, bf16[128,3584]{1,0:T(8,128)(2,1)} %tokens.1, bf16[1,3584,1024]{2,1,0:T(8,128)(2,1)} %w_gate.1, ...), custom_call_target="tpu_custom_call" | custom-call | flops 28185722880 | bytes 52428800 | tf_op jit(solution)/shard_map/moe/pallas_call | solution.py:428
  119.0 0.9 copy.12
  119.9 0.6 copy.13
